TPU v7x, 16 devices: a 4x2x1 block of a 4x4x8 slice. The times are simulated.
16 devices in a mesh: data: 2 (over y, z), ctx: 8 (over x, core).
Axes of the slice: x: 4, y: 2, z: 1, core: 2. Of those that a mesh axis runs over, the one named last changes fastest.
The devices are a block of a 4x4x8 slice.
Arguments:
- hidden: bfloat16 [512, 4096], P(('data', 'ctx')), parts along dimension 0
- seq_lens: int32 [512], P(('data', 'ctx')), parts along dimension 0
- w_query: bfloat16 [4, 4096, 4096], replicated
- w_key: bfloat16 [4, 4096, 1024], replicated
- w_value: bfloat16 [4, 4096, 1024], replicated
- w_out: bfloat16 [4, 4096, 4096], replicated
- k_prefix: bfloat16 [4, 8192, 8, 128], P(None, ('data', 'ctx')), parts along dimension 1
- v_prefix: bfloat16 [4, 8192, 8, 128], P(None, ('data', 'ctx')), parts along dimension 1
- k_suffix: bfloat16 [4, 512, 32, 8, 128], P(None, ('data', 'ctx')), parts along dimension 1
- v_suffix: bfloat16 [4, 512, 32, 8, 128], P(None, ('data', 'ctx')), parts along dimension 1
Outputs:
- output 1: bfloat16 [512, 4096], P(('data', 'ctx')), parts along dimension 0
- output 2: bfloat16 [4, 512, 32, 8, 128], P(None, ('data', 'ctx')), parts along dimension 1
- output 3: bfloat16 [4, 512, 32, 8, 128], P(None, ('data', 'ctx')), parts along dimension 1
There are 2 independent parts. A program takes and returns all parts, laid end to end along the dimension named above; an argument that names none is the same for every part.
All inputs are finite; a program needn't handle non-finite values.
Results may differ from a plain program's by a relative error of at most 0.0139564.
Values are sent between devices in bfloat16 or wider.
A program may use at most 768 MiB of HBM per device.

v0:
```python
import jax
import jax.numpy as jnp
from jax import lax
from jax.sharding import PartitionSpec as P


def solution(mesh):
    ctx_size = mesh.shape['ctx']
    home_axes = ('data', 'ctx')
    row_spec = P(home_axes, None)
    lens_spec = P(home_axes)
    whole_spec = P()
    prefix_spec = P(None, home_axes, None, None)
    cache_spec = P(None, home_axes, None, None, None)

    def local_step(hidden, seq_lens, w_query, w_key, w_value, w_out, k_prefix, v_prefix, k_suffix, v_suffix):
        layers = w_query.shape[0]
        kv_heads = k_prefix.shape[2]
        head_dim = k_prefix.shape[3]
        num_heads = w_query.shape[2] // head_dim
        group_size = num_heads // kv_heads
        home_rows = hidden.shape[0]
        slot_count = k_suffix.shape[2]
        score_scale = head_dim ** -0.5
        slot_ids = lax.broadcasted_iota(jnp.int32, (home_rows, slot_count), 1)
        slot_hit = (slot_ids == seq_lens[:, None])[:, :, None, None]
        slot_live = (slot_ids <= seq_lens[:, None])[:, None, None, :]
        k_layers = []
        v_layers = []
        for layer_idx in range(layers):
            queries = jnp.dot(hidden, w_query[layer_idx], preferred_element_type=jnp.float32).astype(jnp.bfloat16).reshape(home_rows, kv_heads, group_size, head_dim)
            k_new = jnp.dot(hidden, w_key[layer_idx], preferred_element_type=jnp.float32).astype(jnp.bfloat16).reshape(home_rows, 1, kv_heads, head_dim)
            v_new = jnp.dot(hidden, w_value[layer_idx], preferred_element_type=jnp.float32).astype(jnp.bfloat16).reshape(home_rows, 1, kv_heads, head_dim)
            k_cache = jnp.where(slot_hit, k_new, k_suffix[layer_idx])
            v_cache = jnp.where(slot_hit, v_new, v_suffix[layer_idx])
            k_layers.append(k_cache)
            v_layers.append(v_cache)
            group_queries = lax.all_gather(queries, 'ctx', axis=0, tiled=True)
            pre_scores = jnp.einsum('bkgd,pkd->bkgp', group_queries, k_prefix[layer_idx], preferred_element_type=jnp.float32) * score_scale
            pre_max = pre_scores.max(axis=-1)
            pre_exp = jnp.exp(pre_scores - pre_max[..., None])
            pre_mass = pre_exp.sum(axis=-1)
            pre_vals = jnp.einsum('bkgp,pkd->bkgd', pre_exp.astype(jnp.bfloat16), v_prefix[layer_idx], preferred_element_type=jnp.float32)
            part_out = (pre_vals / pre_mass[..., None]).astype(jnp.bfloat16)
            part_lse = pre_max + jnp.log(pre_mass)
            home_out = lax.all_to_all(part_out, 'ctx', 0, 0, tiled=True).reshape(ctx_size, home_rows, kv_heads, group_size, head_dim)
            home_lse = lax.all_to_all(part_lse, 'ctx', 0, 0, tiled=True).reshape(ctx_size, home_rows, kv_heads, group_size)
            suf_scores = jnp.einsum('bkgd,bskd->bkgs', queries, k_cache, preferred_element_type=jnp.float32) * score_scale
            suf_scores = jnp.where(slot_live, suf_scores, -jnp.inf)
            suf_max = suf_scores.max(axis=-1)
            suf_exp = jnp.exp(suf_scores - suf_max[..., None])
            suf_mass = suf_exp.sum(axis=-1)
            suf_vals = jnp.einsum('bkgs,bskd->bkgd', suf_exp.astype(jnp.bfloat16), v_cache, preferred_element_type=jnp.float32)
            row_max = jnp.maximum(home_lse.max(axis=0), suf_max)
            part_weight = jnp.exp(home_lse - row_max)
            suf_weight = jnp.exp(suf_max - row_max)
            mass_sum = part_weight.sum(axis=0) + suf_weight * suf_mass
            mixed_sum = (part_weight[..., None] * home_out.astype(jnp.float32)).sum(axis=0) + suf_weight[..., None] * suf_vals
            attended = (mixed_sum / mass_sum[..., None]).astype(jnp.bfloat16).reshape(home_rows, num_heads * head_dim)
            update = jnp.dot(attended, w_out[layer_idx], preferred_element_type=jnp.float32).astype(jnp.bfloat16)
            hidden = (hidden.astype(jnp.float32) + update.astype(jnp.float32)).astype(jnp.bfloat16)
        return hidden, jnp.stack(k_layers), jnp.stack(v_layers)

    return jax.shard_map(local_step, mesh=mesh, in_specs=(row_spec, lens_spec, whole_spec, whole_spec, whole_spec, whole_spec, prefix_spec, prefix_spec, cache_spec, cache_spec), out_specs=(row_spec, cache_spec, cache_spec), check_vma=False)
```

profile of v0, /device:TPU:113, one launch (start us, length us, event | category | flops | bytes accessed | tf_op | source)
XLA Modules:
  0.0 481.1 jit_solution(292843471272892407)
XLA Ops:
  7.2 13.6 %fusion.76 = bf16[32,4096]{1,0:T(8,128)(2,1)S(1)} fusion(bf16[32,4096]{1,0:T(8,128)(2,1)} %param.10, bf16[4,4096,4096]{2,1,0:T(8,128)(2,1)} %param.12), kind=kOutput, calls=%fused_computation.82 | convolution fusion | flops 1073872896 | bytes 34078720 | tf_op jit(solution)/shard_map/dot_general | solution.py:31
  27.6 4.9 %fusion.258 = bf16[4,8,8,128]{3,1,2,0:T(8,128)(2,1)S(1)} fusion(bf16[32,4096]{1,0:T(8,128)(2,1)S(1)} %copy-done.41, bf16[4,4096,1024]{2,1,0:T(8,128)(2,1)} %param.14), kind=kOutput, calls=%fused_computation.180 | convolution fusion | flops 268468224 | bytes 8716288 | tf_op jit(solution)/shard_map/dot_general | solution.py:33
  32.5 13.8 %all-gather.5.cloned.1.call-done = bf16[256,8,4,128]{3,0,2,1:T(8,128)(2,1)} async-done(((bf16[32,8,4,128]{3,0,2,1:T(8,128)(2,1)}), bf16[256,8,4,128]{3,0,2,1:T(8,128)(2,1)}) %all-gather.5.cloned.1.call-update) | async-done | bytes 2097168 | tf_op jit(solution)/shard_map/all_gather | solution.py:38
  61.6 8.6 %fusion.139 = bf16[256,8,4,128]{3,0,2,1:T(8,128)(2,1)S(1)} fusion(f32[8,256,4,512]{3,1,2,0:T(8,128)} %copy-done.1, f32[256,8,4]{0,2,1:T(4,128)S(1)} %get-tuple-element.49, f32[256,8,4]{0,2,1:T(4,128)S(1)} %fusion.29, bf16[1,512,8,128]{3,2,1,0:T(8,128)(2,1)S(1)} %get-tuple-element.30), kind=kOutput, calls=%fused_computation.109 | convolution fusion | flops 1088421888 | bytes 19988480 | tf_op jit(solution)/shard_map/bkgp,pkd->bkgd/dot_general | solution.py:43
  73.8 4.8 %all-to-all-start.1 = ((bf16[256,8,4,128]{3,2,1,0:T(4,128)(2,1)}), bf16[256,8,4,128]{3,2,1,0:T(4,128)(2,1)S(1)}, u32[]{:S(2)}, u32[]{:S(2)}) async-start(bf16[256,8,4,128]{3,2,1,0:T(4,128)(2,1)} %copy.171), calls=%async_computation.1 | async-start | bytes 4194304 | tf_op jit(solution)/shard_map/all_to_all | solution.py:46
  78.6 5.0 %fusion.261 = bf16[4,8,8,128]{3,1,2,0:T(8,128)(2,1)S(1)} fusion(bf16[32,4096]{1,0:T(8,128)(2,1)} %param.10, bf16[4,4096,1024]{2,1,0:T(8,128)(2,1)} %param.13), kind=kOutput, calls=%fused_computation.181 | convolution fusion | flops 268468224 | bytes 8716288 | tf_op jit(solution)/shard_map/dot_general | solution.py:32
  109.9 13.6 %fusion.88 = bf16[32,4096]{1,0:T(8,128)(2,1)S(1)} fusion(bf16[32,4096]{1,0:T(8,128)(2,1)S(1)} %reshape.228, bf16[4,4096,4096]{2,1,0:T(8,128)(2,1)} %param.15, bf16[32,4096]{1,0:T(8,128)(2,1)S(1)} %copy-done.42), kind=kOutput, calls=%fused_computation.86 | convolution fusion | flops 1074397184 | bytes 34340864 | tf_op jit(solution)/shard_map/dot_general | solution.py:60
  123.5 14.1 %fusion.91 = bf16[32,4096]{1,0:T(8,128)(2,1)S(1)} fusion(bf16[32,4096]{1,0:T(8,128)(2,1)S(1)} %fusion.88, bf16[4,4096,4096]{2,1,0:T(8,128)(2,1)} %param.12), kind=kOutput, calls=%fused_computation.87 | convolution fusion | flops 1073872896 | bytes 34078720 | tf_op jit(solution)/shard_map/dot_general | solution.py:31
  138.7 5.0 %fusion.252 = bf16[4,8,8,128]{3,1,2,0:T(8,128)(2,1)S(1)} fusion(bf16[32,4096]{1,0:T(8,128)(2,1)S(1)} %fusion.88, bf16[4,4096,1024]{2,1,0:T(8,128)(2,1)} %param.14), kind=kOutput, calls=%fused_computation.178 | convolution fusion | flops 268468224 | bytes 8716288 | tf_op jit(solution)/shard_map/dot_general | solution.py:33
  143.7 16.6 %all-gather.7.cloned.1.call-done = bf16[256,8,4,128]{3,0,2,1:T(8,128)(2,1)} async-done(((bf16[32,8,4,128]{3,0,2,1:T(8,128)(2,1)}), bf16[256,8,4,128]{3,0,2,1:T(8,128)(2,1)}) %all-gather.7.cloned.1.call-update) | async-done | bytes 2097168 | tf_op jit(solution)/shard_map/all_gather | solution.py:38
  175.4 8.5 %fusion.138 = bf16[256,8,4,128]{3,0,2,1:T(8,128)(2,1)S(1)} fusion(f32[8,256,4,512]{3,1,2,0:T(8,128)} %copy-done.2, f32[256,8,4]{0,2,1:T(4,128)S(1)} %get-tuple-element.53, f32[256,8,4]{0,2,1:T(4,128)S(1)} %fusion.31, bf16[1,512,8,128]{3,2,1,0:T(8,128)(2,1)S(1)} %copy-done.12), kind=kOutput, calls=%fused_computation.107 | convolution fusion | flops 1088421888 | bytes 19988480 | tf_op jit(solution)/shard_map/bkgp,pkd->bkgd/dot_general | solution.py:43
  186.9 4.8 %all-to-all-start.3 = ((bf16[256,8,4,128]{3,2,1,0:T(4,128)(2,1)}), bf16[256,8,4,128]{3,2,1,0:T(4,128)(2,1)S(1)}, u32[]{:S(2)}, u32[]{:S(2)}) async-start(bf16[256,8,4,128]{3,2,1,0:T(4,128)(2,1)} %copy.190), calls=%async_computation.3 | async-start | bytes 4194304 | tf_op jit(solution)/shard_map/all_to_all | solution.py:46
  191.7 5.0 %fusion.255 = bf16[4,8,8,128]{3,1,2,0:T(8,128)(2,1)S(1)} fusion(bf16[32,4096]{1,0:T(8,128)(2,1)} %copy-done.47, bf16[4,4096,1024]{2,1,0:T(8,128)(2,1)} %param.13), kind=kOutput, calls=%fused_computation.179 | convolution fusion | flops 268468224 | bytes 8716288 | tf_op jit(solution)/shard_map/dot_general | solution.py:32
  196.8 4.9 %bitcast_select_fusion.5 = (bf16[32,32,8,128]{3,2,1,0:T(8,128)(2,1)S(1)}, bf16[32,32,8,128]{3,2,1,0:T(8,128)(2,1)}) fusion(pred[32,32]{1,0:T(8,128)(4,1)S(1)} %get-tuple-element.48, bf16[4,32,32,8,128]{4,3,2,1,0:T(8,128)(2,1)} %param.18, bf16[32,8,128]{2,1,0:T(8,128)(2,1)S(1)} %bitcast.358, bf16[4,32,32,8,128]{4,3,2,1,0:T(8,128)(2,1)} %param.19, ...), kind=kLoop, calls=%fused_computation.123 | loop fusion | flops 2097152 | bytes 8520704 | tf_op jit(solution)/shard_map/jit(_where)/select_n | solution.py:34
  223.1 13.6 %fusion.103 = bf16[32,4096]{1,0:T(8,128)(2,1)S(1)} fusion(bf16[32,4096]{1,0:T(8,128)(2,1)S(1)} %reshape.231, bf16[4,4096,4096]{2,1,0:T(8,128)(2,1)} %param.15, bf16[32,4096]{1,0:T(8,128)(2,1)S(1)} %copy-done.48), kind=kOutput, calls=%fused_computation.91 | convolution fusion | flops 1074397184 | bytes 34340864 | tf_op jit(solution)/shard_map/dot_general | solution.py:60
  236.7 13.9 %fusion.106 = bf16[32,4096]{1,0:T(8,128)(2,1)S(1)} fusion(bf16[32,4096]{1,0:T(8,128)(2,1)S(1)} %fusion.103, bf16[4,4096,4096]{2,1,0:T(8,128)(2,1)} %param.12), kind=kOutput, calls=%fused_computation.92 | convolution fusion | flops 1073872896 | bytes 34078720 | tf_op jit(solution)/shard_map/dot_general | solution.py:31
  251.6 4.9 %fusion.246 = bf16[4,8,8,128]{3,1,2,0:T(8,128)(2,1)S(1)} fusion(bf16[32,4096]{1,0:T(8,128)(2,1)S(1)} %fusion.103, bf16[4,4096,1024]{2,1,0:T(8,128)(2,1)} %param.14), kind=kOutput, calls=%fused_computation.176 | convolution fusion | flops 268468224 | bytes 8716288 | tf_op jit(solution)/shard_map/dot_general | solution.py:33
  257.2 16.4 %all-gather.9.cloned.1.call-done = bf16[256,8,4,128]{3,0,2,1:T(8,128)(2,1)} async-done(((bf16[32,8,4,128]{3,0,2,1:T(8,128)(2,1)}), bf16[256,8,4,128]{3,0,2,1:T(8,128)(2,1)}) %all-gather.9.cloned.1.call-update) | async-done | bytes 2097168 | tf_op jit(solution)/shard_map/all_gather | solution.py:38
  288.8 8.5 %fusion.137 = bf16[256,8,4,128]{3,0,2,1:T(8,128)(2,1)S(1)} fusion(f32[8,256,4,512]{3,1,2,0:T(8,128)} %copy-done.3, f32[256,8,4]{0,2,1:T(4,128)S(1)} %get-tuple-element.57, f32[256,8,4]{0,2,1:T(4,128)S(1)} %fusion.33, bf16[1,512,8,128]{3,2,1,0:T(8,128)(2,1)S(1)} %copy-done.11), kind=kOutput, calls=%fused_computation.105 | convolution fusion | flops 1088421888 | bytes 19988480 | tf_op jit(solution)/shard_map/bkgp,pkd->bkgd/dot_general | solution.py:43
  305.1 5.0 %fusion.249 = bf16[4,8,8,128]{3,1,2,0:T(8,128)(2,1)S(1)} fusion(bf16[32,4096]{1,0:T(8,128)(2,1)S(1)} %copy-done.45, bf16[4,4096,1024]{2,1,0:T(8,128)(2,1)} %param.13), kind=kOutput, calls=%fused_computation.177 | convolution fusion | flops 268468224 | bytes 8716288 | tf_op jit(solution)/shard_map/dot_general | solution.py:32
  310.1 5.2 %bitcast_select_fusion.3 = (bf16[32,32,8,128]{3,2,1,0:T(8,128)(2,1)S(1)}, bf16[32,32,8,128]{3,2,1,0:T(8,128)(2,1)}) fusion(pred[32,32]{1,0:T(8,128)(4,1)S(1)} %get-tuple-element.48, bf16[4,32,32,8,128]{4,3,2,1,0:T(8,128)(2,1)} %param.18, bf16[32,8,128]{2,1,0:T(8,128)(2,1)S(1)} %bitcast.362, bf16[4,32,32,8,128]{4,3,2,1,0:T(8,128)(2,1)} %param.19, ...), kind=kLoop, calls=%fused_computation.121 | loop fusion | flops 2097152 | bytes 8520704 | tf_op jit(solution)/shard_map/jit(_where)/select_n | solution.py:34
  319.6 11.4 %all-to-all-done.5 = bf16[256,8,4,128]{3,2,1,0:T(4,128)(2,1)S(1)} async-done(((bf16[256,8,4,128]{3,2,1,0:T(4,128)(2,1)}), bf16[256,8,4,128]{3,2,1,0:T(4,128)(2,1)S(1)}, u32[]{:S(2)}, u32[]{:S(2)}) %all-to-all-start.5) | async-done | bytes 2097184 | tf_op jit(solution)/shard_map/all_to_all | solution.py:46
  336.4 13.6 %fusion.118 = bf16[32,4096]{1,0:T(8,128)(2,1)S(1)} fusion(bf16[32,4096]{1,0:T(8,128)(2,1)S(1)} %reshape.234, bf16[4,4096,4096]{2,1,0:T(8,128)(2,1)} %param.15, bf16[32,4096]{1,0:T(8,128)(2,1)S(1)} %copy-done.46), kind=kOutput, calls=%fused_computation.96 | convolution fusion | flops 1074397184 | bytes 34340864 | tf_op jit(solution)/shard_map/dot_general | solution.py:60
  350.0 13.8 %fusion.121 = bf16[32,4096]{1,0:T(8,128)(2,1)S(1)} fusion(bf16[32,4096]{1,0:T(8,128)(2,1)S(1)} %fusion.118, bf16[4,4096,4096]{2,1,0:T(8,128)(2,1)} %param.12), kind=kOutput, calls=%fused_computation.97 | convolution fusion | flops 1073872896 | bytes 34078720 | tf_op jit(solution)/shard_map/dot_general | solution.py:31
  364.9 4.9 %fusion.240 = bf16[4,8,8,128]{3,1,2,0:T(8,128)(2,1)S(1)} fusion(bf16[32,4096]{1,0:T(8,128)(2,1)S(1)} %fusion.118, bf16[4,4096,1024]{2,1,0:T(8,128)(2,1)} %param.14), kind=kOutput, calls=%fused_computation.174 | convolution fusion | flops 268468224 | bytes 8716288 | tf_op jit(solution)/shard_map/dot_general | solution.py:33
  369.8 4.9 %fusion.243 = bf16[4,8,8,128]{3,1,2,0:T(8,128)(2,1)S(1)} fusion(bf16[32,4096]{1,0:T(8,128)(2,1)S(1)} %fusion.118, bf16[4,4096,1024]{2,1,0:T(8,128)(2,1)} %param.13), kind=kOutput, calls=%fused_computation.175 | convolution fusion | flops 268468224 | bytes 8716288 | tf_op jit(solution)/shard_map/dot_general | solution.py:32
  383.2 11.1 %broadcast_select_fusion.3 = (bf16[1,32,32,8,128]{4,3,2,1,0:T(8,128)(2,1)S(1)}, bf16[1,32,32,8,128]{4,3,2,1,0:T(8,128)(2,1)}, bf16[1,32,32,8,128]{4,3,2,1,0:T(8,...) fusion(pred[32,32]{1,0:T(8,128)(4,1)S(1)} %get-tuple-element.48, ...), kind=kLoop, calls=%fused_computation.145 | loop fusion | flops 8388608 | bytes 34079744 | tf_op jit(solution)/shard_map/jit(_where)/select_n | solution.py:35
  410.4 8.9 %fusion.136 = bf16[256,8,4,128]{3,0,2,1:T(8,128)(2,1)S(1)} fusion(f32[8,256,4,512]{3,1,2,0:T(8,128)} %copy-done, f32[256,8,4]{0,2,1:T(4,128)S(1)} %get-tuple-element.61, f32[256,8,4]{0,2,1:T(4,128)S(1)} %fusion.35, bf16[1,512,8,128]{3,2,1,0:T(8,128)(2,1)} %get-tuple-element.27), kind=kOutput, calls=%fused_computation.103 | convolution fusion | flops 1088421888 | bytes 19988480 | tf_op jit(solution)/shard_map/bkgp,pkd->bkgd/dot_general | solution.py:43
  422.2 4.9 %all-to-all-start.7 = ((bf16[256,8,4,128]{3,2,1,0:T(4,128)(2,1)}), bf16[256,8,4,128]{3,2,1,0:T(4,128)(2,1)}, u32[]{:S(2)}, u32[]{:S(2)}) async-start(bf16[256,8,4,128]{3,2,1,0:T(4,128)(2,1)} %copy.228), calls=%async_computation.7 | async-start | bytes 4194304 | tf_op jit(solution)/shard_map/all_to_all | solution.py:46
  427.1 11.2 %pad_maximum_fusion = (bf16[4,32,32,8,128]{4,3,2,1,0:T(8,128)(2,1)}, bf16[4,32,32,8,128]{4,3,2,1,0:T(8,128)(2,1)}) fusion(bf16[1,32,32,8,128]{4,3,2,1,0:T(8,128)(2,1)} %get-tuple-element.35, bf16[1,32,32,8,128]{4,3,2,1,0:T(8,128)(2,1)} %get-tuple-element.36, bf16[1,32,32,8,128]{4,3,2,1,0:T(8,128)(2,1)} %get-tuple-element.37, ...), kind=kLoop, calls=%fused_computation.48 | loop fusion | flops 25165824 | bytes 33554432 | tf_op jit(solution)/shard_map/stack | solution.py:62
  440.4 12.8 %all-to-all-done.7 = bf16[256,8,4,128]{3,2,1,0:T(4,128)(2,1)} async-done(((bf16[256,8,4,128]{3,2,1,0:T(4,128)(2,1)}), bf16[256,8,4,128]{3,2,1,0:T(4,128)(2,1)}, u32[]{:S(2)}, u32[]{:S(2)}) %all-to-all-start.7) | async-done | bytes 2097184 | tf_op jit(solution)/shard_map/all_to_all | solution.py:46
  460.0 14.4 %fusion.133 = bf16[32,4096]{1,0:T(8,128)(2,1)} fusion(bf16[32,4096]{1,0:T(8,128)(2,1)S(1)} %reshape.237, bf16[4,4096,4096]{2,1,0:T(8,128)(2,1)} %param.15, bf16[32,4096]{1,0:T(8,128)(2,1)} %copy-done.43), kind=kOutput, calls=%fused_computation.101 | convolution fusion | flops 1074397184 | bytes 34340864 | tf_op jit(solution)/shard_map/dot_general | solution.py:60
  (240 shorter events, 163.5 us)
Async XLA Ops:
  7.2 39.2 %all-gather.5.cloned.1.call-start = ((), (), s32[]{:S(2)}) async-start(), calls=%async_computation.8 | async-start | bytes 2359296 | tf_op jit(solution)/shard_map/all_gather | solution.py:38
  50.4 5.7 %copy-start.1 = (f32[8,256,4,512]{3,1,2,0:T(8,128)}, f32[8,256,4,512]{3,1,2,0:T(8,128)S(1)}, u32[]{:S(2)}) copy-start(f32[8,256,4,512]{3,1,2,0:T(8,128)S(1)} %get-tuple-element.50) | copy-start | bytes 50331652
  57.5 15.6 %all-to-all-start = ((f32[8,1,1024]{2,1,0:T(1,128)}), f32[8,1,1024]{2,1,0:T(1,128)S(1)}, u32[]{:S(2)}, u32[]{:S(2)}) async-start(f32[8,1,1024]{2,1,0:T(1,128)} %reshape.250), calls=%async_computation | async-start | bytes 65536 | tf_op jit(solution)/shard_map/all_to_all | solution.py:47
  73.8 30.8 %all-to-all-start.1 = ((bf16[256,8,4,128]{3,2,1,0:T(4,128)(2,1)}), bf16[256,8,4,128]{3,2,1,0:T(4,128)(2,1)S(1)}, u32[]{:S(2)}, u32[]{:S(2)}) async-start(bf16[256,8,4,128]{3,2,1,0:T(4,128)(2,1)} %copy.171), calls=%async_computation.1 | async-start | bytes 4194304 | tf_op jit(solution)/shard_map/all_to_all | solution.py:46
  78.6 5.1 %copy-start.40 = (s32[32]{0:T(128)S(1)}, s32[32]{0:T(128)}, u32[]{:S(2)}) copy-start(s32[32]{0:T(128)} %param.11) | copy-start | bytes 388
  78.6 81.7 %all-gather.7.cloned.1.call-start = ((), (), s32[]{:S(2)}) async-start(), calls=%async_computation.9 | async-start | bytes 2359296 | tf_op jit(solution)/shard_map/all_gather | solution.py:38
  123.5 15.1 %copy-start.47 = (bf16[32,4096]{1,0:T(8,128)(2,1)}, bf16[32,4096]{1,0:T(8,128)(2,1)S(1)}, u32[]{:S(2)}) copy-start(bf16[32,4096]{1,0:T(8,128)(2,1)S(1)} %fusion.88) | copy-start | bytes 786436
  138.7 21.6 %copy-start.5 = (bf16[1,512,8,128]{3,2,1,0:T(8,128)(2,1)S(1)}, bf16[1,512,8,128]{3,2,1,0:T(8,128)(2,1)}, u32[]{:S(2)}) copy-start(bf16[1,512,8,128]{3,2,1,0:T(8,128)(2,1)} %get-tuple-element.33) | copy-start | bytes 3145732
  164.3 5.9 %copy-start.2 = (f32[8,256,4,512]{3,1,2,0:T(8,128)}, f32[8,256,4,512]{3,1,2,0:T(8,128)S(1)}, u32[]{:S(2)}) copy-start(f32[8,256,4,512]{3,1,2,0:T(8,128)S(1)} %get-tuple-element.54) | copy-start | bytes 50331652
  164.3 11.1 %copy-start.12 = (bf16[1,512,8,128]{3,2,1,0:T(8,128)(2,1)S(1)}, bf16[1,512,8,128]{3,2,1,0:T(8,128)(2,1)}, u32[]{:S(2)}) copy-start(bf16[1,512,8,128]{3,2,1,0:T(8,128)(2,1)} %get-tuple-element.29) | copy-start | bytes 3145732
  171.6 15.3 %all-to-all-start.2 = ((f32[8,1,1024]{2,1,0:T(1,128)}), f32[8,1,1024]{2,1,0:T(1,128)S(1)}, u32[]{:S(2)}, u32[]{:S(2)}) async-start(f32[8,1,1024]{2,1,0:T(1,128)} %reshape.252), calls=%async_computation.2 | async-start | bytes 65536 | tf_op jit(solution)/shard_map/all_to_all | solution.py:47
  186.9 30.8 %all-to-all-start.3 = ((bf16[256,8,4,128]{3,2,1,0:T(4,128)(2,1)}), bf16[256,8,4,128]{3,2,1,0:T(4,128)(2,1)S(1)}, u32[]{:S(2)}, u32[]{:S(2)}) async-start(bf16[256,8,4,128]{3,2,1,0:T(4,128)(2,1)} %copy.190), calls=%async_computation.3 | async-start | bytes 4194304 | tf_op jit(solution)/shard_map/all_to_all | solution.py:46
  191.7 81.9 %all-gather.9.cloned.1.call-start = ((), (), s32[]{:S(2)}) async-start(), calls=%async_computation.10 | async-start | bytes 2359296 | tf_op jit(solution)/shard_map/all_gather | solution.py:38
  236.7 14.9 %copy-start.44 = (bf16[32,4096]{1,0:T(8,128)(2,1)}, bf16[32,4096]{1,0:T(8,128)(2,1)S(1)}, u32[]{:S(2)}) copy-start(bf16[32,4096]{1,0:T(8,128)(2,1)S(1)} %fusion.103) | copy-start | bytes 786436
  277.7 5.9 %copy-start.3 = (f32[8,256,4,512]{3,1,2,0:T(8,128)}, f32[8,256,4,512]{3,1,2,0:T(8,128)S(1)}, u32[]{:S(2)}) copy-start(f32[8,256,4,512]{3,1,2,0:T(8,128)S(1)} %get-tuple-element.58) | copy-start | bytes 50331652
  277.7 11.1 %copy-start.11 = (bf16[1,512,8,128]{3,2,1,0:T(8,128)(2,1)S(1)}, bf16[1,512,8,128]{3,2,1,0:T(8,128)(2,1)}, u32[]{:S(2)}) copy-start(bf16[1,512,8,128]{3,2,1,0:T(8,128)(2,1)} %get-tuple-element.28) | copy-start | bytes 3145732
  285.0 15.3 %all-to-all-start.4 = ((f32[8,1,1024]{2,1,0:T(1,128)}), f32[8,1,1024]{2,1,0:T(1,128)S(1)}, u32[]{:S(2)}, u32[]{:S(2)}) async-start(f32[8,1,1024]{2,1,0:T(1,128)} %reshape.254), calls=%async_computation.4 | async-start | bytes 65536 | tf_op jit(solution)/shard_map/all_to_all | solution.py:47
  297.3 7.8 %copy-start.45 = (bf16[32,4096]{1,0:T(8,128)(2,1)S(1)}, bf16[32,4096]{1,0:T(8,128)(2,1)}, u32[]{:S(2)}) copy-start(bf16[32,4096]{1,0:T(8,128)(2,1)} %copy-done.44) | copy-start | bytes 786436
  300.3 30.8 %all-to-all-start.5 = ((bf16[256,8,4,128]{3,2,1,0:T(4,128)(2,1)}), bf16[256,8,4,128]{3,2,1,0:T(4,128)(2,1)S(1)}, u32[]{:S(2)}, u32[]{:S(2)}) async-start(bf16[256,8,4,128]{3,2,1,0:T(4,128)(2,1)} %copy.209), calls=%async_computation.5 | async-start | bytes 4194304 | tf_op jit(solution)/shard_map/all_to_all | solution.py:46
  305.1 89.3 %all-gather.11.cloned.1.call-start = ((), (), s32[]{:S(2)}) async-start(), calls=%async_computation.11 | async-start | bytes 2359296 | tf_op jit(solution)/shard_map/all_gather | solution.py:38
  310.1 5.2 %copy-start.19 = (bf16[4,8,8,128]{3,2,1,0:T(8,128)(2,1)}, bf16[4,8,8,128]{3,2,1,0:T(8,128)(2,1)S(1)}, u32[]{:S(2)}) copy-start(bf16[4,8,8,128]{3,2,1,0:T(8,128)(2,1)S(1)} %copy.265) | copy-start | bytes 196612
  319.6 15.3 %copy-start.28 = (f32[32,8,4,32]{3,2,1,0:T(4,128)S(1)}, f32[32,8,4,32]{3,2,1,0:T(4,128)}, u32[]{:S(2)}) copy-start(f32[32,8,4,32]{3,2,1,0:T(4,128)} %copy-done.27) | copy-start | bytes 393220
  350.0 19.8 %copy-start.43 = (bf16[32,4096]{1,0:T(8,128)(2,1)}, bf16[32,4096]{1,0:T(8,128)(2,1)S(1)}, u32[]{:S(2)}) copy-start(bf16[32,4096]{1,0:T(8,128)(2,1)S(1)} %fusion.118) | copy-start | bytes 786436
  383.2 11.2 %copy-start.4 = (bf16[1,512,8,128]{3,2,1,0:T(8,128)(2,1)S(1)}, bf16[1,512,8,128]{3,2,1,0:T(8,128)(2,1)}, u32[]{:S(2)}) copy-start(bf16[1,512,8,128]{3,2,1,0:T(8,128)(2,1)} %get-tuple-element.31) | copy-start | bytes 3145732
  398.4 5.7 %copy-start = (f32[8,256,4,512]{3,1,2,0:T(8,128)}, f32[8,256,4,512]{3,1,2,0:T(8,128)S(1)}, u32[]{:S(2)}) copy-start(f32[8,256,4,512]{3,1,2,0:T(8,128)S(1)} %get-tuple-element.62) | copy-start | bytes 50331652
  405.6 16.6 %all-to-all-start.6 = ((f32[8,1,1024]{2,1,0:T(1,128)}), f32[8,1,1024]{2,1,0:T(1,128)S(1)}, u32[]{:S(2)}, u32[]{:S(2)}) async-start(f32[8,1,1024]{2,1,0:T(1,128)} %reshape.256), calls=%async_computation.6 | async-start | bytes 65536 | tf_op jit(solution)/shard_map/all_to_all | solution.py:47
  422.2 31.0 %all-to-all-start.7 = ((bf16[256,8,4,128]{3,2,1,0:T(4,128)(2,1)}), bf16[256,8,4,128]{3,2,1,0:T(4,128)(2,1)}, u32[]{:S(2)}, u32[]{:S(2)}) async-start(bf16[256,8,4,128]{3,2,1,0:T(4,128)(2,1)} %copy.228), calls=%async_computation.7 | async-start | bytes 4194304 | tf_op jit(solution)/shard_map/all_to_all | solution.py:46
  427.1 12.9 %copy-start.32 = (f32[32,8,4]{0,1,2:T(8,128)S(1)}, f32[32,8,4]{0,1,2:T(8,128)}, u32[]{:S(2)}) copy-start(f32[32,8,4]{0,1,2:T(8,128)} %copy.224) | copy-start | bytes 12292
  427.1 13.0 %copy-start.39 = (f32[32,8,4]{0,1,2:T(8,128)S(1)}, f32[32,8,4]{0,1,2:T(8,128)}, u32[]{:S(2)}) copy-start(f32[32,8,4]{0,1,2:T(8,128)} %copy.234) | copy-start | bytes 12292
  440.4 18.3 %copy-start.7 = (bf16[32,32,8,128]{3,2,1,0:T(8,128)(2,1)S(1)}, bf16[32,32,8,128]{3,2,1,0:T(8,128)(2,1)}, u32[]{:S(2)}) copy-start(bf16[32,32,8,128]{3,2,1,0:T(8,128)(2,1)} %get-tuple-element.40) | copy-start | bytes 6291460
  440.4 18.3 %copy-start.24 = (f32[32,8,4,32]{3,2,1,0:T(4,128)S(1)}, f32[32,8,4,32]{3,2,1,0:T(4,128)}, u32[]{:S(2)}) copy-start(f32[32,8,4,32]{3,2,1,0:T(4,128)} %copy-done.23) | copy-start | bytes 393220
  440.4 18.3 %copy-start.30 = (f32[32,8,4]{2,1,0:T(8,128)S(1)}, f32[32,8,4]{2,1,0:T(8,128)}, u32[]{:S(2)}) copy-start(f32[32,8,4]{2,1,0:T(8,128)} %copy-done.29) | copy-start | bytes 12292
  (29 other events, 98.3 us)
Sparse Core Ops, SparseCore 0:
  22.0 24.2 all-gather.4
  138.8 21.4 all-gather.6
  251.7 21.8 all-gather.8
  365.0 21.4 all-gather.10
where the time goes:
time: 490 us; the launch traced here: 481 us
  matrix products  213 us (43%)
  other arithmetic  90.2 us (18%)
  waiting for transfers between devices  73.9 us (15%)
  local copies, waits for them, and re-layouts  53.5 us (11%)
  starting transfers between devices  35.8 us (7%)
  between operations  15 us (3%)
    dot_general x4, matrix products, local_step(): jnp.dot(hidden, w_query[layer_idx], preferred_element_type=jnp.float32)  55.4 us
    dot_general x4, matrix products, local_step(): jnp.dot(attended, w_out[layer_idx], preferred_element_type=jnp.float32)  55.1 us
    all_gather x4, waiting for transfers between devices, local_step(): group_queries = lax.all_gather(queries, 'ctx', axis=0, tiled=True)  46.8 us
    dot_general x4, matrix products, local_step(): jnp.einsum('bkgp,pkd->bkgd', pre_exp.astype(jnp.bfloat16), v_prefix[layer...  34.5 us
    all_to_all x4, waiting for transfers between devices, local_step(): lax.all_to_all(part_out, 'ctx', 0, 0, tiled=True)  26.9 us
    dot_general x4, matrix products, local_step(): jnp.dot(hidden, w_key[layer_idx], preferred_element_type=jnp.float32)  20 us
    dot_general x4, matrix products, local_step(): jnp.dot(hidden, w_value[layer_idx], preferred_element_type=jnp.float32)  19.8 us
    select_n x4, other arithmetic, local_step(): k_cache = jnp.where(slot_hit, k_new, k_suffix[layer_idx])  19.6 us
  transfers between devices with their start and end apart: 12, of which 7 were waited for; matrix products, arithmetic and copies ran while one was open for 36% of the time, Pallas kernels for 0%

commit v1 on v0

v1 whole, which is shorter than its diff:
```python
import functools
import math

import jax
import jax.numpy as jnp
from jax import lax
from jax.experimental import pallas as pl
from jax.experimental.pallas import tpu as pltpu
from jax.sharding import PartitionSpec as P

MESH = pl.DeviceIdType.MESH
F32 = jnp.float32
BF16 = jnp.bfloat16
NEG = -1e30


def decode_kernel(cfg, lens_ref, hid_ref, wq, wk, wv, wo, kp, vp, ks, vs,
                  out_ref, kn_ref, vn_ref,
                  wbuf, xbuf, qkv, qx, qall, raw, kf, kvsrc, kvbuf, sfx, sscr, osend, lsend, orecv, lrecv,
                  q3, n3, o3, l3, obuf,
                  w_sem, raw_sem, sfx_sem, x0_sem, q_ssem, q_rsem, qx_sem, kv_ssem, kv_rsem,
                  o_ssem, o_rsem, l_ssem, l_rsem, ob_sem, x_ssem, x_rsem):
    n_ctx, layers, rows, dim, kvh, grp, hd, pos, slots, nslot, ch = cfg
    chips = n_ctx // 2
    qw = grp * hd
    half_q = chips * qw
    half_kv = chips * hd
    xw = dim // (2 * chips)
    steps = 2 * chips + 2
    total = layers * steps
    scale = hd ** -0.5
    me = lax.axis_index('ctx')
    p = me // 2
    c = me % 2
    mate = 2 * p + (1 - c)
    my_head = chips * c + p
    my_rows = pl.ds(pl.multiple_of(c * rows, rows), rows)
    mate_rows = pl.ds(pl.multiple_of((1 - c) * rows, rows), rows)

    def owner_at(t):
        return (p + lax.rem(t + chips // 2, chips)) % chips if not isinstance(t, int) else (p + (t + chips // 2) % chips) % chips

    def issue_weights(g):
        lyr = g // steps
        j = g % steps
        slot = g % nslot

        @pl.when(g < total)
        def _():
            @pl.when(j < chips)
            def _():
                dest = (p + (j + chips // 2) % chips) % chips
                off = pl.multiple_of(c * half_q + dest * qw, 128)
                pltpu.make_async_copy(wq.at[lyr, :, pl.ds(off, qw)], wbuf.at[slot], w_sem.at[slot]).start()

            @pl.when(j == chips)
            def _():
                off = pl.multiple_of(c * half_kv, 128)
                pltpu.make_async_copy(wk.at[lyr, :, pl.ds(off, half_kv)], wbuf.at[slot], w_sem.at[slot]).start()

            @pl.when(j == chips + 1)
            def _():
                off = pl.multiple_of(c * half_kv, 128)
                pltpu.make_async_copy(wv.at[lyr, :, pl.ds(off, half_kv)], wbuf.at[slot], w_sem.at[slot]).start()

            @pl.when(j > chips + 1)
            def _():
                off = pl.multiple_of(c * (dim // 2) + (j - chips - 2) * xw, 128)
                pltpu.make_async_copy(wo.at[lyr, :, pl.ds(off, xw)], wbuf.at[slot], w_sem.at[slot]).start()

    def wait_weights(g):
        slot = g % nslot
        pltpu.make_async_copy(wq.at[0, :, pl.ds(0, qw)], wbuf.at[slot], w_sem.at[slot]).wait()
        return slot

    def raw_copies(lyr):
        return (pltpu.make_async_copy(kp.at[lyr], raw.at[0], raw_sem.at[0]),
                pltpu.make_async_copy(vp.at[lyr], raw.at[1], raw_sem.at[1]))

    def wait_kv_sent(slot):
        for t in range(2):
            full = kvsrc.at[slot, t, pl.ds(0, n_ctx - 1)]
            pltpu.make_async_remote_copy(full, full, kv_ssem.at[slot, t], kv_rsem.at[0, 0],
                                         device_id={'ctx': mate}, device_id_type=MESH).wait_send()

    def prep_kv(lyr):
        slot = lyr % 2
        for cp in raw_copies(lyr):
            cp.wait()
        blk = 64
        for t in range(2):
            def step(r, _):
                kf[...] = raw[t, pl.ds(pl.multiple_of(r * blk * kvh, 16), blk * kvh), :].astype(F32)
                for h in range(kvh):
                    kvsrc[slot, t, h, pl.ds(pl.multiple_of(r * blk, blk), blk), :] = kf[pl.ds(h, blk, stride=kvh), :].astype(BF16)
                return 0
            lax.fori_loop(0, pos // blk, step, 0)
            kvbuf[lyr, t, pl.ds(pl.multiple_of(me * pos, pos), pos), :] = kvsrc[slot, t, my_head]

        @pl.when(lyr + 1 < layers)
        def _():
            for cp in raw_copies(lyr + 1):
                cp.start()

    def send_kv(lyr):
        slot = lyr % 2
        for j in range(1, n_ctx):
            dest = (me + j) % n_ctx
            head = chips * (dest % 2) + dest // 2
            for t in range(2):
                pltpu.make_async_remote_copy(
                    kvsrc.at[slot, t, head], kvbuf.at[lyr, t, pl.ds(pl.multiple_of(me * pos, pos), pos)],
                    kv_ssem.at[slot, t], kv_rsem.at[lyr, t], device_id={'ctx': dest}, device_id_type=MESH).start()

    def wait_kv(lyr):
        for t in range(2):
            part = kvbuf.at[lyr, t, pl.ds(0, (n_ctx - 1) * pos)]
            pltpu.make_async_remote_copy(part, part, kv_ssem.at[0, 0], kv_rsem.at[lyr, t],
                                         device_id={'ctx': mate}, device_id_type=MESH).wait_recv()

    def sfx_copies(lyr):
        return (pltpu.make_async_copy(ks.at[lyr], sfx.at[0], sfx_sem.at[0]),
                pltpu.make_async_copy(vs.at[lyr], sfx.at[1], sfx_sem.at[1]))

    for cp in raw_copies(0):
        cp.start()
    for g in range(nslot):
        issue_weights(jnp.int32(g))
    for cp in sfx_copies(0):
        cp.start()
    barrier = pltpu.get_barrier_semaphore()
    for j in range(1, n_ctx):
        pl.semaphore_signal(barrier, inc=1, device_id={'ctx': (me + j) % n_ctx}, device_id_type=MESH)
    xbuf[0, my_rows, :] = hid_ref[...]
    pl.semaphore_wait(barrier, n_ctx - 1)
    x0 = pltpu.make_async_remote_copy(xbuf.at[0, my_rows], xbuf.at[0, my_rows], x0_sem.at[0], x0_sem.at[1],
                                      device_id={'ctx': mate}, device_id_type=MESH)
    x0.start()
    prep_kv(jnp.int32(0))
    send_kv(jnp.int32(0))
    x0.wait()

    def q_copy(dest):
        return pltpu.make_async_remote_copy(qkv.at[dest], qall.at[p], q_ssem.at[dest], q_rsem.at[p],
                                            device_id={'ctx': 2 * dest + c}, device_id_type=MESH)

    def q_recv(src):
        return pltpu.make_async_remote_copy(qkv.at[src], qall.at[src], q_ssem.at[src], q_rsem.at[src],
                                            device_id={'ctx': mate}, device_id_type=MESH)

    def o_copy(dest, cc):
        return pltpu.make_async_remote_copy(osend.at[dest, cc], orecv.at[my_head], o_ssem.at[dest, cc], o_rsem.at[my_head],
                                            device_id={'ctx': 2 * dest + cc}, device_id_type=MESH)

    def l_copy(dest, cc):
        return pltpu.make_async_remote_copy(lsend.at[dest, cc], lrecv.at[my_head], l_ssem.at[dest, cc], l_rsem.at[my_head],
                                            device_id={'ctx': 2 * dest + cc}, device_id_type=MESH)

    def layer(lyr, _):
        cur = lyr % 2
        nxt = 1 - cur
        base = lyr * steps

        def proj(t, _):
            g = base + t
            slot = wait_weights(g)
            val = jnp.dot(xbuf[cur], wbuf[slot], preferred_element_type=F32).astype(BF16)
            dest = jnp.where(t < chips, (p + (t + chips // 2) % chips) % chips, t)
            qkv[dest] = val

            @pl.when(t < chips)
            def _():
                @pl.when(dest != p)
                def _():
                    q_copy(dest).start()

                @pl.when(dest == p)
                def _():
                    qall[p] = val
            issue_weights(g + nslot)
            return 0

        lax.fori_loop(0, chips + 2, proj, 0)
        qx_cp = pltpu.make_async_remote_copy(qkv.at[:, mate_rows], qx, qx_sem.at[0], qx_sem.at[1],
                                             device_id={'ctx': mate}, device_id_type=MESH)
        qx_cp.start()

        @pl.when(lyr + 1 < layers)
        def _():
            @pl.when(lyr >= 1)
            def _():
                wait_kv_sent((lyr + 1) % 2)
            prep_kv(lyr + 1)

        wait_kv(lyr)

        def attend(t, _):
            src = (p + (t + 1) % chips) % chips

            @pl.when(src != p)
            def _():
                q_recv(src).wait_recv()
            qv = jnp.concatenate([qall[src, cc * rows:(cc + 1) * rows, g * hd:(g + 1) * hd]
                                  for cc in range(2) for g in range(grp)], axis=0)
            n_rows = 2 * grp * rows
            mx = jnp.full((n_rows, hd), NEG, F32)
            for j in range(n_ctx * pos // ch):
                s = lax.dot_general(qv, kvbuf[lyr, 0, j * ch:(j + 1) * ch, :], (((1,), (1,)), ((), ())), preferred_element_type=F32)
                sscr[:, j * ch:(j + 1) * ch] = s
                for b in range(ch // hd):
                    mx = jnp.maximum(mx, s[:, b * hd:(b + 1) * hd])
            m = mx.max(axis=-1, keepdims=True)
            acc = jnp.zeros((n_rows, hd), F32)
            ls = jnp.zeros((n_rows, hd), F32)
            for j in range(n_ctx * pos // ch):
                e = jnp.exp((sscr[:, j * ch:(j + 1) * ch] - m) * scale)
                for b in range(ch // hd):
                    ls = ls + e[:, b * hd:(b + 1) * hd]
                acc = acc + jnp.dot(e.astype(BF16), kvbuf[lyr, 1, j * ch:(j + 1) * ch, :], preferred_element_type=F32)
            mass = ls.sum(axis=-1, keepdims=True)
            o = (acc / mass).astype(BF16)
            lse = jnp.broadcast_to(m * scale + jnp.log(mass), (n_rows, hd))
            per = grp * rows
            for cc in range(2):
                dev = 2 * src + cc
                for g in range(grp):
                    osend[src, cc, :, g * hd:(g + 1) * hd] = o[cc * per + g * rows: cc * per + (g + 1) * rows]
                lsend[src, cc] = jnp.transpose(lse[cc * per:(cc + 1) * per])[0:8]

                @pl.when(dev != me)
                def _():
                    o_copy(src, cc).start()
                    l_copy(src, cc).start()

                @pl.when(dev == me)
                def _():
                    orecv[my_head] = osend[src, cc]
                    lrecv[my_head] = lsend[src, cc]
            return 0

        lax.fori_loop(0, chips, attend, 0)

        @pl.when(lyr + 1 < layers)
        def _():
            send_kv(lyr + 1)

        qx_cp.wait_recv()
        mine = c * 1
        for h in range(kvh):
            own = mine == h // chips
            hh = h % chips
            for g in range(grp):
                sel = jnp.where(own, qkv[hh, my_rows, g * hd:(g + 1) * hd].astype(F32), qx[hh, :, g * hd:(g + 1) * hd].astype(F32))
                q3[pl.ds(h * grp + g, rows, stride=kvh * grp), :] = sel
            for t in range(2):
                sel = jnp.where(own, qkv[chips + t, my_rows, hh * hd:(hh + 1) * hd].astype(F32), qx[chips + t, :, hh * hd:(hh + 1) * hd].astype(F32))
                n3[t, pl.ds(h, rows, stride=kvh), :] = sel
                (kn_ref, vn_ref)[t][lyr, :, h * hd:(h + 1) * hd] = sel.astype(BF16)
        for cp in sfx_copies(lyr):
            cp.wait()
        nh = kvh * grp
        cols = slots * kvh
        row_slot = lax.broadcasted_iota(jnp.int32, (cols, hd), 0) // kvh
        col_id = lax.broadcasted_iota(jnp.int32, (nh, cols), 1)
        row_id = lax.broadcasted_iota(jnp.int32, (nh, cols), 0)
        same = (col_id % kvh) == (row_id // grp)
        col_slot = jnp.where(same, col_id // kvh, slots + 1)
        unroll = 4

        def suffix(i, _):
            for u in range(unroll):
                b = i * unroll + u
                ln = lens_ref[b]
                hit = row_slot == ln
                kv = []
                for t in range(2):
                    new = n3[t, pl.ds(pl.multiple_of(b * kvh, kvh), kvh), :]
                    new = jnp.broadcast_to(new[None], (slots, kvh, hd)).reshape(cols, hd)
                    kv.append(jnp.where(hit, new, sfx[t, b].astype(F32)).astype(BF16))
                at = pl.ds(pl.multiple_of(b * nh, nh), nh)
                s = lax.dot_general(q3[at, :].astype(BF16), kv[0], (((1,), (1,)), ((), ())), preferred_element_type=F32) * scale
                s = jnp.where(col_slot <= ln, s, -jnp.inf)
                m = s.max(axis=-1, keepdims=True)
                e = jnp.exp(s - m)
                mass = e.sum(axis=-1, keepdims=True)
                o3[at, :] = jnp.dot(e.astype(BF16), kv[1], preferred_element_type=F32) / mass
                l3[at, :] = jnp.broadcast_to(m + jnp.log(mass), (nh, hd))
            return 0

        lax.fori_loop(0, rows // unroll, suffix, 0)

        @pl.when(lyr + 1 < layers)
        def _():
            for cp in sfx_copies(lyr + 1):
                cp.start()

        for h in range(kvh):
            @pl.when(my_head != h)
            def _():
                pltpu.make_async_remote_copy(osend.at[0, 0], orecv.at[h], o_ssem.at[0, 0], o_rsem.at[h],
                                             device_id={'ctx': mate}, device_id_type=MESH).wait_recv()
                pltpu.make_async_remote_copy(lsend.at[0, 0], lrecv.at[h], l_ssem.at[0, 0], l_rsem.at[h],
                                             device_id={'ctx': mate}, device_id_type=MESH).wait_recv()
            lp = jnp.transpose(jnp.concatenate([lrecv[h]] * (hd // 8), axis=0))
            for g in range(grp):
                lpg = lp[g * rows:(g + 1) * rows]
                hx = h * grp + g
                ls = l3[pl.ds(hx, rows, stride=kvh * grp), :]
                os = o3[pl.ds(hx, rows, stride=kvh * grp), :]
                top = jnp.maximum(lpg, ls)
                wp = jnp.exp(lpg - top)
                ws = jnp.exp(ls - top)
                mix = (wp * orecv[h, :, g * hd:(g + 1) * hd].astype(F32) + ws * os) / (wp + ws)
                obuf[my_rows, hx * hd:(hx + 1) * hd] = mix.astype(BF16)
        ob = pltpu.make_async_remote_copy(obuf.at[my_rows], obuf.at[my_rows], ob_sem.at[0], ob_sem.at[1],
                                          device_id={'ctx': mate}, device_id_type=MESH)
        ob.start()
        ob.wait_recv()

        def x_copy(n):
            col = pl.ds(pl.multiple_of(c * (dim // 2) + n * xw, 128), xw)
            return pltpu.make_async_remote_copy(xbuf.at[nxt, :, col], xbuf.at[nxt, :, col], x_ssem.at[n], x_rsem.at[n],
                                                device_id={'ctx': mate}, device_id_type=MESH)

        def outp(n, _):
            g = base + chips + 2 + n
            slot = wait_weights(g)
            upd = jnp.dot(obuf[...], wbuf[slot], preferred_element_type=F32).astype(BF16)
            col = pl.ds(pl.multiple_of(c * (dim // 2) + n * xw, 128), xw)
            xbuf[nxt, :, col] = (xbuf[cur, :, col].astype(F32) + upd.astype(F32)).astype(BF16)
            x_copy(n).start()
            issue_weights(g + nslot)
            return 0

        lax.fori_loop(0, chips, outp, 0)

        qx_cp.wait_send()
        ob.wait_send()
        for t in range(chips):
            @pl.when(p != t)
            def _():
                q_copy(jnp.int32(t)).wait_send()
            for cc in range(2):
                @pl.when(me != 2 * t + cc)
                def _():
                    o_copy(t, cc).wait_send()
                    l_copy(t, cc).wait_send()
        for n in range(chips):
            x_copy(n).wait()
        return 0

    lax.fori_loop(0, layers, layer, 0)
    for back in range(min(2, layers)):
        wait_kv_sent((layers - 1 - back) % 2)
    out_ref[...] = xbuf[layers % 2, my_rows, :]


def solution(mesh):
    n_ctx = mesh.shape['ctx']
    home_axes = ('data', 'ctx')
    row_spec = P(home_axes, None)
    lens_spec = P(home_axes)
    whole_spec = P()
    prefix_spec = P(None, home_axes, None, None)
    cache_spec = P(None, home_axes, None, None, None)

    def local_step(hidden, seq_lens, w_query, w_key, w_value, w_out, k_prefix, v_prefix, k_suffix, v_suffix):
        layers, pos, kvh, hd = k_prefix.shape
        rows, dim = hidden.shape
        slots = k_suffix.shape[2]
        grp = w_query.shape[2] // (kvh * hd)
        chips = n_ctx // 2
        qw = grp * hd
        nslot = 7
        ch = min(1024, n_ctx * pos)
        cfg = (n_ctx, layers, rows, dim, kvh, grp, hd, pos, slots, nslot, ch)
        assert kvh == n_ctx and chips * hd == qw and dim // n_ctx == qw and grp * rows == hd
        nh = kvh * grp
        vmem, anys, smem = pltpu.VMEM, pl.ANY, pltpu.SMEM
        hidden_out, k_new, v_new = pl.pallas_call(
            functools.partial(decode_kernel, cfg),
            out_shape=(jax.ShapeDtypeStruct((rows, dim), BF16),
                       jax.ShapeDtypeStruct((layers, rows, kvh * hd), BF16),
                       jax.ShapeDtypeStruct((layers, rows, kvh * hd), BF16)),
            in_specs=[pl.BlockSpec(memory_space=smem), pl.BlockSpec(memory_space=vmem)] + [pl.BlockSpec(memory_space=anys)] * 8,
            out_specs=[pl.BlockSpec(memory_space=vmem)] * 3,
            scratch_shapes=[
                vmem((nslot, dim, qw), BF16),
                vmem((2, 2 * rows, dim), BF16),
                vmem((chips + 2, 2 * rows, qw), BF16),
                vmem((chips + 2, rows, qw), BF16),
                vmem((chips, 2 * rows, qw), BF16),
                vmem((2, pos * kvh, hd), BF16),
                vmem((64 * kvh, hd), F32),
                vmem((2, 2, kvh, pos, hd), BF16),
                vmem((layers, 2, n_ctx * pos, hd), BF16),
                vmem((2, rows, slots * kvh, hd), BF16),
                vmem((2 * grp * rows, n_ctx * pos), F32),
                vmem((chips, 2, rows, qw), BF16),
                vmem((chips, 2, 8, hd), F32),
                vmem((kvh, rows, qw), BF16),
                vmem((kvh, 8, hd), F32),
                vmem((rows * nh, hd), F32),
                vmem((2, rows * kvh, hd), F32),
                vmem((rows * nh, hd), F32),
                vmem((rows * nh, hd), F32),
                vmem((2 * rows, nh * hd), BF16),
                pltpu.SemaphoreType.DMA((nslot,)),
                pltpu.SemaphoreType.DMA((2,)),
                pltpu.SemaphoreType.DMA((2,)),
                pltpu.SemaphoreType.DMA((2,)),
                pltpu.SemaphoreType.DMA((chips,)),
                pltpu.SemaphoreType.DMA((chips,)),
                pltpu.SemaphoreType.DMA((2,)),
                pltpu.SemaphoreType.DMA((2, 2)),
                pltpu.SemaphoreType.DMA((layers, 2)),
                pltpu.SemaphoreType.DMA((chips, 2)),
                pltpu.SemaphoreType.DMA((kvh,)),
                pltpu.SemaphoreType.DMA((chips, 2)),
                pltpu.SemaphoreType.DMA((kvh,)),
                pltpu.SemaphoreType.DMA((2,)),
                pltpu.SemaphoreType.DMA((chips,)),
                pltpu.SemaphoreType.DMA((chips,)),
            ],
            compiler_params=pltpu.CompilerParams(collective_id=0, has_side_effects=True, vmem_limit_bytes=67043328),
            name='decode_layers',
        )(seq_lens, hidden, w_query, w_key, w_value, w_out,
          k_prefix.reshape(layers, pos * kvh, hd), v_prefix.reshape(layers, pos * kvh, hd),
          k_suffix.reshape(layers, rows, slots * kvh, hd), v_suffix.reshape(layers, rows, slots * kvh, hd))
        hit = (lax.broadcasted_iota(jnp.int32, (rows, slots), 1) == seq_lens[:, None])[None, :, :, None, None]
        k_out = jnp.where(hit, k_new.reshape(layers, rows, 1, kvh, hd), k_suffix)
        v_out = jnp.where(hit, v_new.reshape(layers, rows, 1, kvh, hd), v_suffix)
        return hidden_out, k_out, v_out

    return jax.shard_map(local_step, mesh=mesh, in_specs=(row_spec, lens_spec, whole_spec, whole_spec, whole_spec, whole_spec, prefix_spec, prefix_spec, cache_spec, cache_spec), out_specs=(row_spec, cache_spec, cache_spec), check_vma=False)
```

time: 490 us -> 189 us (0.39); the launches traced: 481 us -> 189 us
  matrix products: 213 us -> 0 us
  Pallas kernels: 0 us -> 172 us
  other arithmetic: 90.2 us -> 13.4 us
  waiting for transfers between devices: 73.9 us -> 0 us
  local copies, waits for them, and re-layouts: 53.5 us -> 2.69 us
  starting transfers between devices: 35.8 us -> 0 us
  between operations: 15 us -> 0.66 us
    dot_general x32 -> x0, matrix products: 213 us -> none  [the longest x4 55.4 us: local_step(): jnp.dot(hidden, w_query[layer_idx], preferred_element_type=jnp.float32)]
    pallas_call x0 -> x1, Pallas kernels: none -> 172 us  [local_step(): pl.pallas_call(functools.partial(decode_kernel, cfg), out_shape=(jax.Shap...]
    all_gather x4 -> x0, waiting for transfers between devices: 46.8 us -> none  [local_step(): group_queries = lax.all_gather(queries, 'ctx', axis=0, tiled=True)]
    all_to_all x8 -> x0, starting transfers between devices: 35.8 us -> none  [the longest x4 19.3 us: local_step(): lax.all_to_all(part_out, 'ctx', 0, 0, tiled=True)]
    reduce_sum x16 -> x0, other arithmetic: 32 us -> none  [the longest x4 16.3 us: local_step(): pre_mass = pre_exp.sum(axis=-1)]
    all_to_all x8 -> x0, waiting for transfers between devices: 26.9 us -> none  [the longest x4 26.9 us: local_step(): lax.all_to_all(part_out, 'ctx', 0, 0, tiled=True)]
    select_n x5 -> x1, other arithmetic: 30.7 us -> 12 us  [local_step(): v_out = jnp.where(hit, v_new.reshape(layers, rows, 1, kvh, hd), v_suffix)]
    unnamed x114 -> x5, local copies, waits for them, and re-layouts: 17.3 us -> 2.69 us
  transfers between devices with their start and end apart: 12 -> 0, of which waited for: 7 -> 0; matrix products, arithmetic and copies ran while one was open for 36% -> 0% of each run, Pallas kernels for 0% -> 0%
where the time goes in v1:
time: 189 us
  Pallas kernels  172 us (91%)
  other arithmetic  13.4 us (7%)
  local copies, waits for them, and re-layouts  2.69 us (1%)
    pallas_call x1, Pallas kernels, local_step(): pl.pallas_call(functools.partial(decode_kernel, cfg), out_shape=(jax.Shap...  172 us
    select_n x1, other arithmetic, local_step(): v_out = jnp.where(hit, v_new.reshape(layers, rows, 1, kvh, hd), v_suffix)  12 us

profile of v1, /device:TPU:113, one launch (start us, length us, event | category | flops | bytes accessed | tf_op | source)
XLA Modules:
  0.0 189.2 jit_solution(14835843756910116529)
XLA Ops:
  0.6 1.3 iota_compare_fusion
  2.0 172.5 %decode_layers.1 = (bf16[32,4096]{1,0:T(8,128)(2,1)}, bf16[4,32,1024]{2,1,0:T(8,128)(2,1)}, bf16[4,32,1024]{2,1,0:T(8,128)(2,1)}) custom-call(s32[32]{0:T(128)} %lens_ref.1, bf16[32,4096]{1,0:T(8,128)(2,1)} %hid_ref.1, bf16[4,4096,4096]{2,1,0:T(8,128)(2,1)} %wq.1, bf16[4,4096,1024]{2,1,0:T(8,128)(2,1)} %wk.1, bf16[4,4096,1024]{2,1,0:T(8,128)(2,1)} %wv.1, ...), custom_call_target="tpu_custom_call" | custom-call | tf_op jit(solution)/shard_map/decode_layers/pallas_call | solution.py:380
  174.4 1.0 copy.13
  175.4 1.0 copy.14
  176.4 0.0 copy-start
  176.4 12.0 %broadcast_select_fusion = (bf16[4,32,32,8,128]{4,3,2,1,0:T(8,128)(2,1)}, bf16[4,32,32,8,128]{4,3,2,1,0:T(8,128)(2,1)}) fusion(bf16[4,32,32,8,128]{4,3,2,1,0:T(8,128)(2,1)} %param.19, pred[32,32]{1,0:T(8,128)(4,1)} %iota_compare_fusion, bf16[4,32,8,128]{3,2,1,0:T(8,128)(2,1)S(1)} %bitcast.17, bf16[4,32,32,8,128]{4,3,2,1,0:T(8,128)(2,1)} %param.18, ...), kind=kLoop, calls=%fused_computation | loop fusion | flops 8388608 | bytes 34079744 | tf_op jit(solution)/shard_map/jit(_where)/select_n | solution.py:432
  188.5 0.0 copy-done
  188.5 0.7 copy.16
Async XLA Ops:
  176.4 12.0 %copy-start = (bf16[32,4096]{1,0:T(8,128)(2,1)S(1)}, bf16[32,4096]{1,0:T(8,128)(2,1)}, u32[]{:S(2)}) copy-start(bf16[32,4096]{1,0:T(8,128)(2,1)} %get-tuple-element.14) | copy-start | bytes 786436

commit v2 on v1

v2 whole, which is shorter than its diff:
```python
import functools
import math

import jax
import jax.numpy as jnp
from jax import lax
from jax.experimental import pallas as pl
from jax.experimental.pallas import tpu as pltpu
from jax.sharding import PartitionSpec as P

MESH = pl.DeviceIdType.MESH
F32 = jnp.float32
BF16 = jnp.bfloat16
NEG = -1e30
UNROLL = 8
EARLY = 2
PACED = False
LOG2E = 1.4426950408889634


def decode_kernel(cfg, lens_ref, hid_ref, wq, wk, wv, wo, kp, vp, ks, vs,
                  out_ref, kn_ref, vn_ref,
                  wbuf, xbuf, qkv, qx, qall, raw, kf, kvsrc, kvbuf, sfx, sscr, osend, lsend, orecv, lrecv,
                  q3, n3, o3, l3, obuf,
                  w_sem, raw_sem, sfx_sem, x0_sem, q_ssem, q_rsem, qx_sem, kv_ssem, kv_rsem,
                  o_ssem, o_rsem, l_ssem, l_rsem, ob_sem, x_ssem, x_rsem):
    n_ctx, layers, rows, dim, kvh, grp, hd, pos, slots, nslot, ch = cfg
    chips = n_ctx // 2
    qw = grp * hd
    half_q = chips * qw
    half_kv = chips * hd
    xw = dim // (2 * chips)
    steps = 2 * chips + 2
    total = layers * steps
    scale = hd ** -0.5
    me = lax.axis_index('ctx')
    p = me // 2
    c = me % 2
    mate = 2 * p + (1 - c)
    far = chips // 2
    my_head = chips * c + p
    far_head = chips * c + (p + far) % chips
    near_len = 6 * pos
    my_rows = pl.ds(pl.multiple_of(c * rows, rows), rows)
    mate_rows = pl.ds(pl.multiple_of((1 - c) * rows, rows), rows)

    def issue_weights(g):
        lyr = g // steps
        j = g % steps
        slot = g % nslot

        @pl.when(g < total)
        def _():
            @pl.when(j < chips)
            def _():
                dest = (p + (j + chips // 2) % chips) % chips
                off = pl.multiple_of(c * half_q + dest * qw, 128)
                pltpu.make_async_copy(wq.at[lyr, :, pl.ds(off, qw)], wbuf.at[slot], w_sem.at[slot]).start()

            @pl.when(j == chips)
            def _():
                off = pl.multiple_of(c * half_kv, 128)
                pltpu.make_async_copy(wk.at[lyr, :, pl.ds(off, half_kv)], wbuf.at[slot], w_sem.at[slot]).start()

            @pl.when(j == chips + 1)
            def _():
                off = pl.multiple_of(c * half_kv, 128)
                pltpu.make_async_copy(wv.at[lyr, :, pl.ds(off, half_kv)], wbuf.at[slot], w_sem.at[slot]).start()

            @pl.when(j > chips + 1)
            def _():
                off = pl.multiple_of(c * (dim // 2) + (j - chips - 2) * xw, 128)
                pltpu.make_async_copy(wo.at[lyr, :, pl.ds(off, xw)], wbuf.at[slot], w_sem.at[slot]).start()

    def wait_weights(g):
        slot = g % nslot
        pltpu.make_async_copy(wq.at[0, :, pl.ds(0, qw)], wbuf.at[slot], w_sem.at[slot]).wait()
        return slot

    def raw_copies(lyr):
        return (pltpu.make_async_copy(kp.at[lyr], raw.at[0], raw_sem.at[0]),
                pltpu.make_async_copy(vp.at[lyr], raw.at[1], raw_sem.at[1]))

    def wait_kv_sent(slot):
        for t in range(2):
            full = kvsrc.at[slot, t, pl.ds(0, 6)]
            pltpu.make_async_remote_copy(full, full, kv_ssem.at[slot, t], kv_rsem.at[0, 0],
                                         device_id={'ctx': mate}, device_id_type=MESH).wait_send()

    def prep_kv(lyr, then=None):
        slot = lyr % 2
        blk = 64
        for t in range(2):
            pltpu.make_async_copy((kp, vp)[t].at[lyr], raw.at[t], raw_sem.at[t]).wait()

            def step(r, _):
                kf[...] = raw[t, pl.ds(pl.multiple_of(r * blk * kvh, 16), blk * kvh), :].astype(F32)
                for h in range(kvh):
                    kvsrc[slot, t, h, pl.ds(pl.multiple_of(r * blk, blk), blk), :] = kf[pl.ds(h, blk, stride=kvh), :].astype(BF16)
                return 0
            lax.fori_loop(0, pos // blk, step, 0)
            kvbuf[lyr, t, pl.ds(pl.multiple_of(c * pos, pos), pos), :] = kvsrc[slot, t, my_head]
            kvbuf[lyr, t, pl.ds(pl.multiple_of((6 + c) * pos, pos), pos), :] = kvsrc[slot, t, far_head]
            if then is not None:
                then(t)

        @pl.when(lyr + 1 < layers)
        def _():
            for cp in raw_copies(lyr + 1):
                cp.start()

    def send_kv(lyr, t, head, place, dev):
        slot = lyr % 2
        pltpu.make_async_remote_copy(
            kvsrc.at[slot, t, head], kvbuf.at[lyr, t, pl.ds(pl.multiple_of((place + c) * pos, pos), pos)],
            kv_ssem.at[slot, t], kv_rsem.at[lyr, t], device_id={'ctx': dev}, device_id_type=MESH).start()

    def send_kv_mate(lyr, t):
        send_kv(lyr, t, chips * (1 - c) + p, 0, mate)
        send_kv(lyr, t, chips * (1 - c) + (p + far) % chips, 6, mate)

    def send_kv_near(lyr, t, cc):
        up = (p + 1) % chips
        down = (p + chips - 1) % chips
        send_kv(lyr, t, chips * cc + up, 2, 2 * up + cc)
        send_kv(lyr, t, chips * cc + down, 4, 2 * down + cc)

    def wait_kv(lyr):
        for t in range(2):
            part = kvbuf.at[lyr, t, pl.ds(0, 6 * pos)]
            pltpu.make_async_remote_copy(part, part, kv_ssem.at[0, 0], kv_rsem.at[lyr, t],
                                         device_id={'ctx': mate}, device_id_type=MESH).wait_recv()

    def sfx_copies(lyr):
        return (pltpu.make_async_copy(ks.at[lyr], sfx.at[0], sfx_sem.at[0]),
                pltpu.make_async_copy(vs.at[lyr], sfx.at[1], sfx_sem.at[1]))

    for cp in raw_copies(0):
        cp.start()
    for g in range(nslot):
        issue_weights(jnp.int32(g))
    for cp in sfx_copies(0):
        cp.start()
    barrier = pltpu.get_barrier_semaphore()
    for j in range(1, n_ctx):
        pl.semaphore_signal(barrier, inc=1, device_id={'ctx': (me + j) % n_ctx}, device_id_type=MESH)
    xbuf[0, my_rows, :] = hid_ref[...]
    pl.semaphore_wait(barrier, n_ctx - 1)
    x0 = pltpu.make_async_remote_copy(xbuf.at[0, my_rows], xbuf.at[0, my_rows], x0_sem.at[0], x0_sem.at[1],
                                      device_id={'ctx': mate}, device_id_type=MESH)
    x0.start()

    def send_first(t):
        for cc in range(2):
            send_kv_near(jnp.int32(0), t, cc)
        send_kv_mate(jnp.int32(0), t)

    prep_kv(jnp.int32(0), send_first)
    x0.wait()

    def q_copy(kind, head):
        dest = (head + far * kind) % chips
        return pltpu.make_async_remote_copy(qkv.at[head], qall.at[kind, p], q_ssem.at[kind, head], q_rsem.at[kind, p],
                                            device_id={'ctx': 2 * dest + c}, device_id_type=MESH)

    def q_recv(kind, src):
        return pltpu.make_async_remote_copy(qkv.at[src], qall.at[kind, src], q_ssem.at[kind, src], q_rsem.at[kind, src],
                                            device_id={'ctx': mate}, device_id_type=MESH)

    def o_copy(kind, dest, cc):
        to = (my_head, far_head)[kind]
        return pltpu.make_async_remote_copy(osend.at[kind, dest, cc], orecv.at[kind, to], o_ssem.at[kind, dest, cc], o_rsem.at[kind, to],
                                            device_id={'ctx': 2 * dest + cc}, device_id_type=MESH)

    def l_copy(kind, dest, cc):
        to = (my_head, far_head)[kind]
        return pltpu.make_async_remote_copy(lsend.at[kind, dest, cc], lrecv.at[kind, to], l_ssem.at[kind, dest, cc], l_rsem.at[kind, to],
                                            device_id={'ctx': 2 * dest + cc}, device_id_type=MESH)

    def layer(lyr, _):
        cur = lyr % 2
        nxt = 1 - cur
        base = lyr * steps

        def proj(t, _):
            g = base + t
            slot = wait_weights(g)
            val = jnp.dot(xbuf[cur], wbuf[slot], preferred_element_type=F32).astype(BF16)
            dest = jnp.where(t < chips, (p + (t + chips // 2) % chips) % chips, t)
            qkv[dest] = val

            @pl.when(t < chips)
            def _():
                for kind in range(2):
                    @pl.when((dest + far * kind) % chips != p)
                    def _():
                        q_copy(kind, dest).start()

                    @pl.when((dest + far * kind) % chips == p)
                    def _():
                        qall[kind, p] = val
            issue_weights(g + nslot)
            return 0

        lax.fori_loop(0, chips + 2, proj, 0)
        qx_cp = pltpu.make_async_remote_copy(qkv.at[:, mate_rows], qx, qx_sem.at[0], qx_sem.at[1],
                                             device_id={'ctx': mate}, device_id_type=MESH)
        qx_cp.start()

        @pl.when(lyr + 1 < layers)
        def _():
            @pl.when(lyr >= 1)
            def _():
                wait_kv_sent((lyr + 1) % 2)
            prep_kv(lyr + 1)

        qx_cp.wait_recv()
        mine = c * 1
        for h in range(kvh):
            own = mine == h // chips
            hh = h % chips
            for g in range(grp):
                sel = jnp.where(own, qkv[hh, my_rows, g * hd:(g + 1) * hd].astype(F32), qx[hh, :, g * hd:(g + 1) * hd].astype(F32))
                q3[pl.ds(h * grp + g, rows, stride=kvh * grp), :] = sel
            for t in range(2):
                sel = jnp.where(own, qkv[chips + t, my_rows, hh * hd:(hh + 1) * hd].astype(F32), qx[chips + t, :, hh * hd:(hh + 1) * hd].astype(F32))
                n3[t, pl.ds(h, rows, stride=kvh), :] = sel
        kn_ref[lyr] = n3[0].astype(BF16)
        vn_ref[lyr] = n3[1].astype(BF16)
        for cp in sfx_copies(lyr):
            cp.wait()
        nh = kvh * grp
        cols = slots * kvh
        slot_id = lax.broadcasted_iota(jnp.int32, (slots, kvh, hd), 0)
        col_id = lax.broadcasted_iota(jnp.int32, (nh, cols), 1)
        row_id = lax.broadcasted_iota(jnp.int32, (nh, cols), 0)
        same = (col_id % kvh) == (row_id // grp)
        col_slot = jnp.where(same, col_id // kvh, slots + 1)
        unroll = UNROLL
        batches = rows // unroll
        early = jnp.where(lyr == 0, batches, EARLY)

        def suffix(i, _):
            bs = [i * unroll + u for u in range(unroll)]
            lns = [lens_ref[b] for b in bs]
            ats = [pl.ds(pl.multiple_of(b * nh, nh), nh) for b in bs]
            kv = []
            for b, ln in zip(bs, lns):
                hit = slot_id == ln
                for t in range(2):
                    new = n3[t, pl.ds(pl.multiple_of(b * kvh, kvh), kvh), :]
                    old = sfx[t, b].astype(F32).reshape(slots, kvh, hd)
                    kv.append(jnp.where(hit, new[None], old).reshape(cols, hd).astype(BF16))
            ss = [lax.dot_general(q3[at, :].astype(BF16), kv[2 * u], (((1,), (1,)), ((), ())), preferred_element_type=F32) * scale
                  for u, at in enumerate(ats)]
            ss = [jnp.where(col_slot <= ln, s, -jnp.inf) for s, ln in zip(ss, lns)]
            ms = [s.max(axis=-1, keepdims=True) for s in ss]
            es = [jnp.exp(s - m) for s, m in zip(ss, ms)]
            sums = [e.sum(axis=-1, keepdims=True) for e in es]
            os = [jnp.dot(e.astype(BF16), kv[2 * u + 1], preferred_element_type=F32) for u, e in enumerate(es)]
            for at, m, mass, o in zip(ats, ms, sums, os):
                o3[at, :] = o / mass
                l3[at, :] = jnp.broadcast_to(m + jnp.log(mass), (nh, hd))
            return 0

        lax.fori_loop(0, early, suffix, 0)


        def attend(kind, lo, hi, t):
            src = (p + (t + 1) % chips) % chips

            @pl.when(src != p)
            def _():
                q_recv(kind, src).wait_recv()
            qv = jnp.concatenate([qall[kind, src, cc * rows:(cc + 1) * rows, g * hd:(g + 1) * hd]
                                  for cc in range(2) for g in range(grp)], axis=0)
            n_rows = 2 * grp * rows
            mx = jnp.full((n_rows, hd), NEG, F32)
            for j in range(lo, hi, ch):
                s = lax.dot_general(qv, kvbuf[lyr, 0, j:j + ch, :], (((1,), (1,)), ((), ())), preferred_element_type=F32)
                sscr[:, j:j + ch] = s
                for b in range(ch // hd):
                    mx = jnp.maximum(mx, s[:, b * hd:(b + 1) * hd])
            m = mx.max(axis=-1, keepdims=True)
            acc = jnp.zeros((n_rows, hd), F32)
            ls = jnp.zeros((n_rows, hd), F32)
            for j in range(lo, hi, ch):
                e = jnp.exp2((sscr[:, j:j + ch] - m) * (scale * LOG2E))
                for b in range(ch // hd):
                    ls = ls + e[:, b * hd:(b + 1) * hd]
                acc = acc + jnp.dot(e.astype(BF16), kvbuf[lyr, 1, j:j + ch, :], preferred_element_type=F32)
            mass = ls.sum(axis=-1, keepdims=True)
            o = (acc / mass).astype(BF16)
            lse = jnp.broadcast_to(m * scale + jnp.log(mass), (n_rows, hd))
            per = grp * rows
            to = (my_head, far_head)[kind]
            for cc in range(2):
                dev = 2 * src + cc
                for g in range(grp):
                    osend[kind, src, cc, :, g * hd:(g + 1) * hd] = o[cc * per + g * rows: cc * per + (g + 1) * rows]
                lsend[kind, src, cc] = jnp.transpose(lse[cc * per:(cc + 1) * per])[0:8]

                @pl.when(dev != me)
                def _():
                    o_copy(kind, src, cc).start()
                    l_copy(kind, src, cc).start()

                @pl.when(dev == me)
                def _():
                    orecv[kind, to] = osend[kind, src, cc]
                    lrecv[kind, to] = lsend[kind, src, cc]

        def attend_far(t, _):
            attend(1, near_len, near_len + 2 * pos, t)
            return 0

        def attend_near(t, _):
            attend(0, 0, near_len, t)
            if PACED:
                @pl.when((lyr + 1 < layers) & (t < 4))
                def _():
                    send_kv_near(lyr + 1, t // 2, t % 2)
            return 0

        wait_kv(lyr)
        lax.fori_loop(0, chips, attend_far, 0)
        lax.fori_loop(0, chips, attend_near, 0)

        @pl.when(lyr + 1 < layers)
        def _():
            for t in range(2):
                if not PACED:
                    for cc in range(2):
                        send_kv_near(lyr + 1, t, cc)
                send_kv_mate(lyr + 1, t)

        lax.fori_loop(early, batches, suffix, 0)

        @pl.when(lyr + 1 < layers)
        def _():
            for cp in sfx_copies(lyr + 1):
                cp.start()

        for h in range(kvh):
            lps = []
            for kind in range(2):
                @pl.when((my_head, far_head)[kind] != h)
                def _():
                    pltpu.make_async_remote_copy(osend.at[0, 0, 0], orecv.at[kind, h], o_ssem.at[0, 0, 0], o_rsem.at[kind, h],
                                                 device_id={'ctx': mate}, device_id_type=MESH).wait_recv()
                    pltpu.make_async_remote_copy(lsend.at[0, 0, 0], lrecv.at[kind, h], l_ssem.at[0, 0, 0], l_rsem.at[kind, h],
                                                 device_id={'ctx': mate}, device_id_type=MESH).wait_recv()
                lps.append(jnp.transpose(jnp.concatenate([lrecv[kind, h]] * (hd // 8), axis=0)))
            for g in range(grp):
                hx = h * grp + g
                la, lb = [lp[g * rows:(g + 1) * rows] for lp in lps]
                ls = l3[pl.ds(hx, rows, stride=kvh * grp), :]
                os = o3[pl.ds(hx, rows, stride=kvh * grp), :]
                top = jnp.maximum(jnp.maximum(la, lb), ls)
                wa = jnp.exp(la - top)
                wb = jnp.exp(lb - top)
                ws = jnp.exp(ls - top)
                mix = (wa * orecv[0, h, :, g * hd:(g + 1) * hd].astype(F32) + wb * orecv[1, h, :, g * hd:(g + 1) * hd].astype(F32)
                       + ws * os) / (wa + wb + ws)
                obuf[my_rows, hx * hd:(hx + 1) * hd] = mix.astype(BF16)
        ob = pltpu.make_async_remote_copy(obuf.at[my_rows], obuf.at[my_rows], ob_sem.at[0], ob_sem.at[1],
                                          device_id={'ctx': mate}, device_id_type=MESH)
        ob.start()
        ob.wait_recv()

        def x_copy(n):
            col = pl.ds(pl.multiple_of(c * (dim // 2) + n * xw, 128), xw)
            return pltpu.make_async_remote_copy(xbuf.at[nxt, :, col], xbuf.at[nxt, :, col], x_ssem.at[n], x_rsem.at[n],
                                                device_id={'ctx': mate}, device_id_type=MESH)

        def outp(n, _):
            g = base + chips + 2 + n
            slot = wait_weights(g)
            upd = jnp.dot(obuf[...], wbuf[slot], preferred_element_type=F32).astype(BF16)
            col = pl.ds(pl.multiple_of(c * (dim // 2) + n * xw, 128), xw)
            xbuf[nxt, :, col] = (xbuf[cur, :, col].astype(F32) + upd.astype(F32)).astype(BF16)
            x_copy(n).start()
            issue_weights(g + nslot)
            return 0

        lax.fori_loop(0, chips, outp, 0)

        qx_cp.wait_send()
        ob.wait_send()
        for kind in range(2):
            for t in range(chips):
                @pl.when(p != (t + far * kind) % chips)
                def _():
                    q_copy(kind, t).wait_send()
                for cc in range(2):
                    @pl.when(me != 2 * t + cc)
                    def _():
                        o_copy(kind, t, cc).wait_send()
                        l_copy(kind, t, cc).wait_send()
        for n in range(chips):
            x_copy(n).wait()
        return 0

    lax.fori_loop(0, layers, layer, 0)
    for back in range(min(2, layers)):
        wait_kv_sent((layers - 1 - back) % 2)
    out_ref[...] = xbuf[layers % 2, my_rows, :]


def insert_kernel(lens_ref, hid_ref, kn_ref, vn_ref, ks_ref, vs_ref, ho_ref, ko_ref, vo_ref,
                  hid, new, buf, h_sem, n_sem, in_sem, out_sem):
    layers, rows = ks_ref.shape[:2]
    sides = ((kn_ref, ks_ref, ko_ref), (vn_ref, vs_ref, vo_ref))
    news = [pltpu.make_async_copy(sides[t][0], new.at[t], n_sem.at[t]) for t in range(2)]
    loads = [(lyr, t, pltpu.make_async_copy(sides[t][1].at[lyr], buf.at[lyr, t], in_sem.at[lyr, t]))
             for lyr in range(layers) for t in range(2)]
    h_in = pltpu.make_async_copy(hid_ref, hid, h_sem.at[0])
    h_out = pltpu.make_async_copy(hid, ho_ref, h_sem.at[1])
    for cp in news:
        cp.start()
    for _, _, cp in loads:
        cp.start()
    h_in.start()
    for cp in news:
        cp.wait()
    stores = []
    for lyr, t, cp in loads:
        cp.wait()
        for b in range(rows):
            buf[lyr, t, b, lens_ref[b]] = new[t, lyr, b]
        out = pltpu.make_async_copy(buf.at[lyr, t], sides[t][2].at[lyr], out_sem.at[lyr, t])
        out.start()
        stores.append(out)
    h_in.wait()
    h_out.start()
    for out in stores:
        out.wait()
    h_out.wait()


def solution(mesh):
    n_ctx = mesh.shape['ctx']
    home_axes = ('data', 'ctx')
    row_spec = P(home_axes, None)
    lens_spec = P(home_axes)
    whole_spec = P()
    prefix_spec = P(None, home_axes, None, None)
    cache_spec = P(None, home_axes, None, None, None)

    def local_step(hidden, seq_lens, w_query, w_key, w_value, w_out, k_prefix, v_prefix, k_suffix, v_suffix):
        layers, pos, kvh, hd = k_prefix.shape
        rows, dim = hidden.shape
        slots = k_suffix.shape[2]
        grp = w_query.shape[2] // (kvh * hd)
        chips = n_ctx // 2
        qw = grp * hd
        nslot = 7
        ch = min(1024, 2 * pos)
        cfg = (n_ctx, layers, rows, dim, kvh, grp, hd, pos, slots, nslot, ch)
        assert chips == 4 and kvh == n_ctx and chips * hd == qw and dim // n_ctx == qw and grp * rows == hd
        nh = kvh * grp
        vmem, anys, smem = pltpu.VMEM, pl.ANY, pltpu.SMEM
        hidden_out, k_new, v_new = pl.pallas_call(
            functools.partial(decode_kernel, cfg),
            out_shape=(jax.ShapeDtypeStruct((rows, dim), BF16),
                       jax.ShapeDtypeStruct((layers, rows * kvh, hd), BF16),
                       jax.ShapeDtypeStruct((layers, rows * kvh, hd), BF16)),
            in_specs=[pl.BlockSpec(memory_space=smem), pl.BlockSpec(memory_space=vmem)] + [pl.BlockSpec(memory_space=anys)] * 8,
            out_specs=[pl.BlockSpec(memory_space=vmem)] * 3,
            scratch_shapes=[
                vmem((nslot, dim, qw), BF16),
                vmem((2, 2 * rows, dim), BF16),
                vmem((chips + 2, 2 * rows, qw), BF16),
                vmem((chips + 2, rows, qw), BF16),
                vmem((2, chips, 2 * rows, qw), BF16),
                vmem((2, pos * kvh, hd), BF16),
                vmem((64 * kvh, hd), F32),
                vmem((2, 2, kvh, pos, hd), BF16),
                vmem((layers, 2, n_ctx * pos, hd), BF16),
                vmem((2, rows, slots * kvh, hd), BF16),
                vmem((2 * grp * rows, n_ctx * pos), F32),
                vmem((2, chips, 2, rows, qw), BF16),
                vmem((2, chips, 2, 8, hd), F32),
                vmem((2, kvh, rows, qw), BF16),
                vmem((2, kvh, 8, hd), F32),
                vmem((rows * nh, hd), F32),
                vmem((2, rows * kvh, hd), F32),
                vmem((rows * nh, hd), F32),
                vmem((rows * nh, hd), F32),
                vmem((2 * rows, nh * hd), BF16),
                pltpu.SemaphoreType.DMA((nslot,)),
                pltpu.SemaphoreType.DMA((2,)),
                pltpu.SemaphoreType.DMA((2,)),
                pltpu.SemaphoreType.DMA((2,)),
                pltpu.SemaphoreType.DMA((2, chips)),
                pltpu.SemaphoreType.DMA((2, chips)),
                pltpu.SemaphoreType.DMA((2,)),
                pltpu.SemaphoreType.DMA((2, 2)),
                pltpu.SemaphoreType.DMA((layers, 2)),
                pltpu.SemaphoreType.DMA((2, chips, 2)),
                pltpu.SemaphoreType.DMA((2, kvh)),
                pltpu.SemaphoreType.DMA((2, chips, 2)),
                pltpu.SemaphoreType.DMA((2, kvh)),
                pltpu.SemaphoreType.DMA((2,)),
                pltpu.SemaphoreType.DMA((chips,)),
                pltpu.SemaphoreType.DMA((chips,)),
            ],
            compiler_params=pltpu.CompilerParams(collective_id=0, has_side_effects=True, vmem_limit_bytes=67043328),
            name='decode_layers',
        )(seq_lens, hidden, w_query, w_key, w_value, w_out,
          k_prefix.reshape(layers, pos * kvh, hd), v_prefix.reshape(layers, pos * kvh, hd),
          k_suffix.reshape(layers, rows, slots * kvh, hd), v_suffix.reshape(layers, rows, slots * kvh, hd))
        hidden_out, k_out, v_out = pl.pallas_call(
            insert_kernel,
            out_shape=(jax.ShapeDtypeStruct((rows, dim), BF16), jax.ShapeDtypeStruct(k_suffix.shape, BF16),
                       jax.ShapeDtypeStruct(v_suffix.shape, BF16)),
            in_specs=[pl.BlockSpec(memory_space=smem)] + [pl.BlockSpec(memory_space=anys)] * 5,
            out_specs=[pl.BlockSpec(memory_space=anys)] * 3,
            scratch_shapes=[
                vmem((rows, dim), BF16),
                vmem((2, layers, rows, kvh, hd), BF16),
                vmem((layers, 2, rows, slots, kvh, hd), BF16),
                pltpu.SemaphoreType.DMA((2,)),
                pltpu.SemaphoreType.DMA((2,)),
                pltpu.SemaphoreType.DMA((layers, 2)),
                pltpu.SemaphoreType.DMA((layers, 2)),
            ],
            compiler_params=pltpu.CompilerParams(vmem_limit_bytes=67043328),
            name='insert_rows',
        )(seq_lens, hidden_out, k_new.reshape(layers, rows, kvh, hd), v_new.reshape(layers, rows, kvh, hd), k_suffix, v_suffix)
        return hidden_out, k_out, v_out

    return jax.shard_map(local_step, mesh=mesh, in_specs=(row_spec, lens_spec, whole_spec, whole_spec, whole_spec, whole_spec, prefix_spec, prefix_spec, cache_spec, cache_spec), out_specs=(row_spec, cache_spec, cache_spec), check_vma=False)
```

time: 189 us -> 149 us (0.79)
  Pallas kernels: 172 us -> 148 us
  other arithmetic: 13.4 us -> 0 us
  local copies, waits for them, and re-layouts: 2.69 us -> 0 us
    pallas_call x1, Pallas kernels: 172 us -> 136 us  [local_step(): pl.pallas_call(functools.partial(decode_kernel, cfg), out_shape=(jax.Shap...]
    select_n x1 -> x0, other arithmetic: 12 us -> none  [local_step(): v_out = jnp.where(hit, v_new.reshape(layers, rows, 1, kvh, hd), v_suffix)]
    pallas_call x0 -> x1, Pallas kernels: none -> 12 us  [local_step(): pl.pallas_call(insert_kernel, out_shape=(jax.ShapeDtypeStruct((rows, dim)...]
    unnamed x5 -> x0, local copies, waits for them, and re-layouts: 2.69 us -> none
where the time goes in v2:
time: 149 us
  Pallas kernels  148 us (99%)
    pallas_call x1, Pallas kernels, local_step(): pl.pallas_call(functools.partial(decode_kernel, cfg), out_shape=(jax.Shap...  136 us
    pallas_call x1, Pallas kernels, local_step(): pl.pallas_call(insert_kernel, out_shape=(jax.ShapeDtypeStruct((rows, dim)...  12 us

profile of v2, /device:TPU:113, one launch (start us, length us, event | category | flops | bytes accessed | tf_op | source)
XLA Modules:
  0.0 148.7 jit_solution(8046250325962593318)
XLA Ops:
  0.6 136.1 %decode_layers.1 = (bf16[32,4096]{1,0:T(8,128)(2,1)}, bf16[4,256,128]{2,1,0:T(8,128)(2,1)}, bf16[4,256,128]{2,1,0:T(8,128)(2,1)}) custom-call(s32[32]{0:T(128)} %lens_ref.3, bf16[32,4096]{1,0:T(8,128)(2,1)} %hid_ref.1, bf16[4,4096,4096]{2,1,0:T(8,128)(2,1)} %wq.1, bf16[4,4096,1024]{2,1,0:T(8,128)(2,1)} %wk.1, bf16[4,4096,1024]{2,1,0:T(8,128)(2,1)} %wv.1, ...), custom_call_target="tpu_custom_call" | custom-call | tf_op jit(solution)/shard_map/decode_layers/pallas_call | solution.py:463
  136.7 12.0 %insert_rows.1 = (bf16[32,4096]{1,0:T(8,128)(2,1)}, bf16[4,32,32,8,128]{4,3,2,1,0:T(8,128)(2,1)}, bf16[4,32,32,8,128]{4,3,2,1,0:T(8,128)(2,1)}) custom-call(s32[32]{0:T(128)} %lens_ref.3, bf16[32,4096]{1,0:T(8,128)(2,1)} %get-tuple-element.6.hid_ref, bf16[4,32,8,128]{3,2,1,0:T(8,128)(2,1)} %bitcast.10, bf16[4,32,8,128]{3,2,1,0:T(8,128)(2,1)} %bitcast.11, ...), custom_call_target="tpu_custom_call" | custom-call | tf_op jit(solution)/shard_map/insert_rows/pallas_call | solution.py:513

commit v3 on v2

--- a/solution.py
+++ b/solution.py
@@ -14,15 +14,15 @@
 NEG = -1e30
 UNROLL = 8
 EARLY = 2
-PACED = False
+CHUNK = 1024
 LOG2E = 1.4426950408889634
 
 
 def decode_kernel(cfg, lens_ref, hid_ref, wq, wk, wv, wo, kp, vp, ks, vs,
                   out_ref, kn_ref, vn_ref,
-                  wbuf, xbuf, qkv, qx, qall, raw, kf, kvsrc, kvbuf, sfx, sscr, osend, lsend, orecv, lrecv,
+                  wbuf, xbuf, qkv, qx, qall, raw, kf, kvsrc, kvbuf, sfx, sscr, mscr, osend, lsend, orecv, lrecv,
                   q3, n3, o3, l3, obuf,
-                  w_sem, raw_sem, sfx_sem, x0_sem, q_ssem, q_rsem, qx_sem, kv_ssem, kv_rsem,
+                  w_sem, raw_sem, sfx_sem, x0_sem, q_ssem, q_rsem, qx_sem, kv_ssem, kv_rsem, kvm_rsem,
                   o_ssem, o_rsem, l_ssem, l_rsem, ob_sem, x_ssem, x_rsem):
     n_ctx, layers, rows, dim, kvh, grp, hd, pos, slots, nslot, ch = cfg
     chips = n_ctx // 2
@@ -81,55 +81,49 @@
         return (pltpu.make_async_copy(kp.at[lyr], raw.at[0], raw_sem.at[0]),
                 pltpu.make_async_copy(vp.at[lyr], raw.at[1], raw_sem.at[1]))
 
-    def wait_kv_sent(slot):
-        for t in range(2):
-            full = kvsrc.at[slot, t, pl.ds(0, 6)]
-            pltpu.make_async_remote_copy(full, full, kv_ssem.at[slot, t], kv_rsem.at[0, 0],
-                                         device_id={'ctx': mate}, device_id_type=MESH).wait_send()
-
-    def prep_kv(lyr, then=None):
+    def wait_kv_sent(slot, t):
+        full = kvsrc.at[slot, t, pl.ds(0, 6)]
+        pltpu.make_async_remote_copy(full, full, kv_ssem.at[slot, t], kv_rsem.at[0, 0],
+                                     device_id={'ctx': mate}, device_id_type=MESH).wait_send()
+
+    def prep_kv(lyr, t):
         slot = lyr % 2
         blk = 64
-        for t in range(2):
-            pltpu.make_async_copy((kp, vp)[t].at[lyr], raw.at[t], raw_sem.at[t]).wait()
-
-            def step(r, _):
-                kf[...] = raw[t, pl.ds(pl.multiple_of(r * blk * kvh, 16), blk * kvh), :].astype(F32)
-                for h in range(kvh):
-                    kvsrc[slot, t, h, pl.ds(pl.multiple_of(r * blk, blk), blk), :] = kf[pl.ds(h, blk, stride=kvh), :].astype(BF16)
-                return 0
-            lax.fori_loop(0, pos // blk, step, 0)
-            kvbuf[lyr, t, pl.ds(pl.multiple_of(c * pos, pos), pos), :] = kvsrc[slot, t, my_head]
-            kvbuf[lyr, t, pl.ds(pl.multiple_of((6 + c) * pos, pos), pos), :] = kvsrc[slot, t, far_head]
-            if then is not None:
-                then(t)
+        pltpu.make_async_copy((kp, vp)[t].at[lyr], raw.at[t], raw_sem.at[t]).wait()
+
+        def step(r, _):
+            kf[...] = raw[t, pl.ds(pl.multiple_of(r * blk * kvh, 16), blk * kvh), :].astype(F32)
+            for h in range(kvh):
+                kvsrc[slot, t, h, pl.ds(pl.multiple_of(r * blk, blk), blk), :] = kf[pl.ds(h, blk, stride=kvh), :].astype(BF16)
+            return 0
+        lax.fori_loop(0, pos // blk, step, 0)
+        kvbuf[lyr, t, pl.ds(pl.multiple_of(c * pos, pos), pos), :] = kvsrc[slot, t, my_head]
+        kvbuf[lyr, t, pl.ds(pl.multiple_of((6 + c) * pos, pos), pos), :] = kvsrc[slot, t, far_head]
 
         @pl.when(lyr + 1 < layers)
         def _():
-            for cp in raw_copies(lyr + 1):
-                cp.start()
-
-    def send_kv(lyr, t, head, place, dev):
+            pltpu.make_async_copy((kp, vp)[t].at[lyr + 1], raw.at[t], raw_sem.at[t]).start()
+
+    def send_kv(lyr, t, head, place, dev, sem):
         slot = lyr % 2
         pltpu.make_async_remote_copy(
             kvsrc.at[slot, t, head], kvbuf.at[lyr, t, pl.ds(pl.multiple_of((place + c) * pos, pos), pos)],
-            kv_ssem.at[slot, t], kv_rsem.at[lyr, t], device_id={'ctx': dev}, device_id_type=MESH).start()
+            kv_ssem.at[slot, t], sem.at[lyr, t], device_id={'ctx': dev}, device_id_type=MESH).start()
 
     def send_kv_mate(lyr, t):
-        send_kv(lyr, t, chips * (1 - c) + p, 0, mate)
-        send_kv(lyr, t, chips * (1 - c) + (p + far) % chips, 6, mate)
+        send_kv(lyr, t, chips * (1 - c) + p, 0, mate, kvm_rsem)
+        send_kv(lyr, t, chips * (1 - c) + (p + far) % chips, 6, mate, kvm_rsem)
 
     def send_kv_near(lyr, t, cc):
         up = (p + 1) % chips
         down = (p + chips - 1) % chips
-        send_kv(lyr, t, chips * cc + up, 2, 2 * up + cc)
-        send_kv(lyr, t, chips * cc + down, 4, 2 * down + cc)
-
-    def wait_kv(lyr):
-        for t in range(2):
-            part = kvbuf.at[lyr, t, pl.ds(0, 6 * pos)]
-            pltpu.make_async_remote_copy(part, part, kv_ssem.at[0, 0], kv_rsem.at[lyr, t],
-                                         device_id={'ctx': mate}, device_id_type=MESH).wait_recv()
+        send_kv(lyr, t, chips * cc + up, 2, 2 * up + cc, kv_rsem)
+        send_kv(lyr, t, chips * cc + down, 4, 2 * down + cc, kv_rsem)
+
+    def wait_kv(lyr, t, sem, count):
+        part = kvbuf.at[lyr, t, pl.ds(0, count * pos)]
+        pltpu.make_async_remote_copy(part, part, kv_ssem.at[0, 0], sem.at[lyr, t],
+                                     device_id={'ctx': mate}, device_id_type=MESH).wait_recv()
 
     def sfx_copies(lyr):
         return (pltpu.make_async_copy(ks.at[lyr], sfx.at[0], sfx_sem.at[0]),
@@ -137,10 +131,7 @@
 
     for cp in raw_copies(0):
         cp.start()
-    for g in range(nslot):
-        issue_weights(jnp.int32(g))
-    for cp in sfx_copies(0):
-        cp.start()
+    issue_weights(jnp.int32(0))
     barrier = pltpu.get_barrier_semaphore()
     for j in range(1, n_ctx):
         pl.semaphore_signal(barrier, inc=1, device_id={'ctx': (me + j) % n_ctx}, device_id_type=MESH)
@@ -149,13 +140,16 @@
     x0 = pltpu.make_async_remote_copy(xbuf.at[0, my_rows], xbuf.at[0, my_rows], x0_sem.at[0], x0_sem.at[1],
                                       device_id={'ctx': mate}, device_id_type=MESH)
     x0.start()
-
-    def send_first(t):
-        for cc in range(2):
-            send_kv_near(jnp.int32(0), t, cc)
+    for t in range(2):
+        prep_kv(jnp.int32(0), t)
+        if t == 0:
+            for g in range(1, nslot):
+                issue_weights(jnp.int32(g))
+            for cc in range(2):
+                send_kv_near(jnp.int32(0), t, cc)
         send_kv_mate(jnp.int32(0), t)
-
-    prep_kv(jnp.int32(0), send_first)
+    for cp in sfx_copies(0):
+        cp.start()
     x0.wait()
 
     def q_copy(kind, head):
@@ -207,12 +201,92 @@
                                              device_id={'ctx': mate}, device_id_type=MESH)
         qx_cp.start()
 
-        @pl.when(lyr + 1 < layers)
+        @pl.when(lyr == 0)
         def _():
-            @pl.when(lyr >= 1)
-            def _():
-                wait_kv_sent((lyr + 1) % 2)
-            prep_kv(lyr + 1)
+            for cc in range(2):
+                send_kv_near(lyr, 1, cc)
+
+        @pl.when((lyr == 0) & (layers > 1))
+        def _():
+            prep_kv(lyr + 1, 0)
+            prep_kv(lyr + 1, 1)
+
+        n_rows = 2 * grp * rows
+        per = grp * rows
+        rate = scale * LOG2E
+
+        def src_at(kind, t):
+            return (p + chips - t) % chips if kind else (p + t + 1) % chips
+
+        def take_q(kind, t):
+            src = src_at(kind, t)
+
+            @pl.when(src != p)
+            def _():
+                q_recv(kind, src).wait_recv()
+            return jnp.concatenate([qall[kind, src, cc * rows:(cc + 1) * rows, g * hd:(g + 1) * hd]
+                                    for cc in range(2) for g in range(grp)], axis=0)
+
+        def block(kind, lo, hi, t, score, value):
+            old = mscr[...] if value else None
+            qv = take_q(kind, t) if score else None
+            if score:
+                mx = jnp.full((n_rows, hd), NEG, F32)
+            if value:
+                acc = jnp.zeros((n_rows, hd), F32)
+                ls = jnp.zeros((n_rows, hd), F32)
+            for j in range(lo, hi, ch):
+                if value:
+                    e = jnp.exp2((sscr[:, j:j + ch] - old[:, 0:1]) * rate)
+                if score:
+                    s = lax.dot_general(qv, kvbuf[lyr, 0, j:j + ch, :], (((1,), (1,)), ((), ())), preferred_element_type=F32)
+                    sscr[:, j:j + ch] = s
+                if value:
+                    for b in range(ch // hd):
+                        ls = ls + e[:, b * hd:(b + 1) * hd]
+                    acc = acc + jnp.dot(e.astype(BF16), kvbuf[lyr, 1, j:j + ch, :], preferred_element_type=F32)
+                if score:
+                    for b in range(ch // hd):
+                        mx = jnp.maximum(mx, s[:, b * hd:(b + 1) * hd])
+            if score:
+                mscr[...] = jnp.broadcast_to(mx.max(axis=-1, keepdims=True), (n_rows, hd))
+            if value:
+                src = src_at(kind, t - 1)
+                to = (my_head, far_head)[kind]
+                mass = ls.sum(axis=-1, keepdims=True)
+                o = (acc / mass).astype(BF16)
+                lse = old * scale + jnp.log(mass)
+                for cc in range(2):
+                    dev = 2 * src + cc
+                    for g in range(grp):
+                        osend[kind, src, cc, :, g * hd:(g + 1) * hd] = o[cc * per + g * rows: cc * per + (g + 1) * rows]
+                    lsend[kind, src, cc] = jnp.transpose(lse[cc * per:(cc + 1) * per])[0:8]
+
+                    @pl.when(dev != me)
+                    def _():
+                        o_copy(kind, src, cc).start()
+                        l_copy(kind, src, cc).start()
+
+                    @pl.when(dev == me)
+                    def _():
+                        orecv[kind, to] = osend[kind, src, cc]
+                        lrecv[kind, to] = lsend[kind, src, cc]
+
+        def attention(kind, first, lo, hi):
+            block(kind, lo, hi, first, True, False)
+
+            def both(t, _):
+                block(kind, lo, hi, t, True, True)
+                return 0
+            lax.fori_loop(first + 1, chips, both, 0)
+            block(kind, lo, hi, chips, False, True)
+
+        far_part = (near_len, near_len + 2 * pos)
+        near_part = (0, near_len)
+        wait_kv(lyr, 0, kvm_rsem, 2)
+        wait_kv(lyr, 1, kvm_rsem, 2)
+        block(1, *far_part, 0, True, False)
+        block(1, *far_part, 1, False, True)
 
         qx_cp.wait_recv()
         mine = c * 1
@@ -266,72 +340,16 @@
         lax.fori_loop(0, early, suffix, 0)
 
 
-        def attend(kind, lo, hi, t):
-            src = (p + (t + 1) % chips) % chips
-
-            @pl.when(src != p)
-            def _():
-                q_recv(kind, src).wait_recv()
-            qv = jnp.concatenate([qall[kind, src, cc * rows:(cc + 1) * rows, g * hd:(g + 1) * hd]
-                                  for cc in range(2) for g in range(grp)], axis=0)
-            n_rows = 2 * grp * rows
-            mx = jnp.full((n_rows, hd), NEG, F32)
-            for j in range(lo, hi, ch):
-                s = lax.dot_general(qv, kvbuf[lyr, 0, j:j + ch, :], (((1,), (1,)), ((), ())), preferred_element_type=F32)
-                sscr[:, j:j + ch] = s
-                for b in range(ch // hd):
-                    mx = jnp.maximum(mx, s[:, b * hd:(b + 1) * hd])
-            m = mx.max(axis=-1, keepdims=True)
-            acc = jnp.zeros((n_rows, hd), F32)
-            ls = jnp.zeros((n_rows, hd), F32)
-            for j in range(lo, hi, ch):
-                e = jnp.exp2((sscr[:, j:j + ch] - m) * (scale * LOG2E))
-                for b in range(ch // hd):
-                    ls = ls + e[:, b * hd:(b + 1) * hd]
-                acc = acc + jnp.dot(e.astype(BF16), kvbuf[lyr, 1, j:j + ch, :], preferred_element_type=F32)
-            mass = ls.sum(axis=-1, keepdims=True)
-            o = (acc / mass).astype(BF16)
-            lse = jnp.broadcast_to(m * scale + jnp.log(mass), (n_rows, hd))
-            per = grp * rows
-            to = (my_head, far_head)[kind]
-            for cc in range(2):
-                dev = 2 * src + cc
-                for g in range(grp):
-                    osend[kind, src, cc, :, g * hd:(g + 1) * hd] = o[cc * per + g * rows: cc * per + (g + 1) * rows]
-                lsend[kind, src, cc] = jnp.transpose(lse[cc * per:(cc + 1) * per])[0:8]
-
-                @pl.when(dev != me)
-                def _():
-                    o_copy(kind, src, cc).start()
-                    l_copy(kind, src, cc).start()
-
-                @pl.when(dev == me)
-                def _():
-                    orecv[kind, to] = osend[kind, src, cc]
-                    lrecv[kind, to] = lsend[kind, src, cc]
-
-        def attend_far(t, _):
-            attend(1, near_len, near_len + 2 * pos, t)
-            return 0
-
-        def attend_near(t, _):
-            attend(0, 0, near_len, t)
-            if PACED:
-                @pl.when((lyr + 1 < layers) & (t < 4))
-                def _():
-                    send_kv_near(lyr + 1, t // 2, t % 2)
-            return 0
-
-        wait_kv(lyr)
-        lax.fori_loop(0, chips, attend_far, 0)
-        lax.fori_loop(0, chips, attend_near, 0)
+        attention(1, 1, *far_part)
+        wait_kv(lyr, 0, kv_rsem, 4)
+        wait_kv(lyr, 1, kv_rsem, 4)
+        attention(0, 0, *near_part)
 
         @pl.when(lyr + 1 < layers)
         def _():
             for t in range(2):
-                if not PACED:
-                    for cc in range(2):
-                        send_kv_near(lyr + 1, t, cc)
+                for cc in range(2):
+                    send_kv_near(lyr + 1, t, cc)
                 send_kv_mate(lyr + 1, t)
 
         lax.fori_loop(early, batches, suffix, 0)
@@ -341,31 +359,44 @@
             for cp in sfx_copies(lyr + 1):
                 cp.start()
 
-        for h in range(kvh):
-            lps = []
-            for kind in range(2):
-                @pl.when((my_head, far_head)[kind] != h)
-                def _():
-                    pltpu.make_async_remote_copy(osend.at[0, 0, 0], orecv.at[kind, h], o_ssem.at[0, 0, 0], o_rsem.at[kind, h],
-                                                 device_id={'ctx': mate}, device_id_type=MESH).wait_recv()
-                    pltpu.make_async_remote_copy(lsend.at[0, 0, 0], lrecv.at[kind, h], l_ssem.at[0, 0, 0], l_rsem.at[kind, h],
-                                                 device_id={'ctx': mate}, device_id_type=MESH).wait_recv()
-                lps.append(jnp.transpose(jnp.concatenate([lrecv[kind, h]] * (hd // 8), axis=0)))
-            for g in range(grp):
-                hx = h * grp + g
-                la, lb = [lp[g * rows:(g + 1) * rows] for lp in lps]
-                ls = l3[pl.ds(hx, rows, stride=kvh * grp), :]
-                os = o3[pl.ds(hx, rows, stride=kvh * grp), :]
-                top = jnp.maximum(jnp.maximum(la, lb), ls)
-                wa = jnp.exp(la - top)
-                wb = jnp.exp(lb - top)
-                ws = jnp.exp(ls - top)
-                mix = (wa * orecv[0, h, :, g * hd:(g + 1) * hd].astype(F32) + wb * orecv[1, h, :, g * hd:(g + 1) * hd].astype(F32)
-                       + ws * os) / (wa + wb + ws)
-                obuf[my_rows, hx * hd:(hx + 1) * hd] = mix.astype(BF16)
+        def arrived(kind, h):
+            @pl.when((my_head, far_head)[kind] != h)
+            def _():
+                pltpu.make_async_remote_copy(osend.at[0, 0, 0], orecv.at[kind, h], o_ssem.at[0, 0, 0], o_rsem.at[kind, h],
+                                             device_id={'ctx': mate}, device_id_type=MESH).wait_recv()
+                pltpu.make_async_remote_copy(lsend.at[0, 0, 0], lrecv.at[kind, h], l_ssem.at[0, 0, 0], l_rsem.at[kind, h],
+                                             device_id={'ctx': mate}, device_id_type=MESH).wait_recv()
+            return jnp.transpose(jnp.concatenate([lrecv[kind, h]] * (hd // 8), axis=0))
+
+        for kind in (1, 0):
+            for h in range(kvh):
+                lp = arrived(kind, h)
+                for g in range(grp):
+                    hx = h * grp + g
+                    at = pl.ds(hx, rows, stride=kvh * grp)
+                    la = lp[g * rows:(g + 1) * rows]
+                    ls = l3[at, :]
+                    top = jnp.maximum(la, ls)
+                    wa = jnp.exp(la - top)
+                    ws = jnp.exp(ls - top)
+                    both_mass = wa + ws
+                    mix = (wa * orecv[kind, h, :, g * hd:(g + 1) * hd].astype(F32) + ws * o3[at, :]) / both_mass
+                    if kind:
+                        o3[at, :] = mix
+                        l3[at, :] = top + jnp.log(both_mass)
+                    else:
+                        obuf[my_rows, hx * hd:(hx + 1) * hd] = mix.astype(BF16)
         ob = pltpu.make_async_remote_copy(obuf.at[my_rows], obuf.at[my_rows], ob_sem.at[0], ob_sem.at[1],
                                           device_id={'ctx': mate}, device_id_type=MESH)
         ob.start()
+
+        def prep_ahead(t):
+            @pl.when(lyr + 2 < layers)
+            def _():
+                wait_kv_sent(lyr % 2, t)
+                prep_kv(lyr + 2, t)
+
+        prep_ahead(0)
         ob.wait_recv()
 
         def x_copy(n):
@@ -384,6 +415,7 @@
             return 0
 
         lax.fori_loop(0, chips, outp, 0)
+        prep_ahead(1)
 
         qx_cp.wait_send()
         ob.wait_send()
@@ -403,7 +435,8 @@
 
     lax.fori_loop(0, layers, layer, 0)
     for back in range(min(2, layers)):
-        wait_kv_sent((layers - 1 - back) % 2)
+        for t in range(2):
+            wait_kv_sent((layers - 1 - back) % 2, t)
     out_ref[...] = xbuf[layers % 2, my_rows, :]
 
 
@@ -455,7 +488,7 @@
         chips = n_ctx // 2
         qw = grp * hd
         nslot = 7
-        ch = min(1024, 2 * pos)
+        ch = min(CHUNK, 2 * pos)
         cfg = (n_ctx, layers, rows, dim, kvh, grp, hd, pos, slots, nslot, ch)
         assert chips == 4 and kvh == n_ctx and chips * hd == qw and dim // n_ctx == qw and grp * rows == hd
         nh = kvh * grp
@@ -479,6 +512,7 @@
                 vmem((layers, 2, n_ctx * pos, hd), BF16),
                 vmem((2, rows, slots * kvh, hd), BF16),
                 vmem((2 * grp * rows, n_ctx * pos), F32),
+                vmem((2 * grp * rows, hd), F32),
                 vmem((2, chips, 2, rows, qw), BF16),
                 vmem((2, chips, 2, 8, hd), F32),
                 vmem((2, kvh, rows, qw), BF16),
@@ -496,6 +530,7 @@
                 pltpu.SemaphoreType.DMA((2, chips)),
                 pltpu.SemaphoreType.DMA((2,)),
                 pltpu.SemaphoreType.DMA((2, 2)),
+                pltpu.SemaphoreType.DMA((layers, 2)),
                 pltpu.SemaphoreType.DMA((layers, 2)),
                 pltpu.SemaphoreType.DMA((2, chips, 2)),
                 pltpu.SemaphoreType.DMA((2, kvh)),

time: 149 us -> 136 us (0.913)
  Pallas kernels: 148 us -> 135 us
    pallas_call x1, Pallas kernels: 136 us -> 123 us  [local_step(): pl.pallas_call(functools.partial(decode_kernel, cfg), out_shape=(jax.Shap...]
where the time goes in v3:
time: 136 us
  Pallas kernels  135 us (99%)
    pallas_call x1, Pallas kernels, local_step(): pl.pallas_call(functools.partial(decode_kernel, cfg), out_shape=(jax.Shap...  123 us
    pallas_call x1, Pallas kernels, local_step(): pl.pallas_call(insert_kernel, out_shape=(jax.ShapeDtypeStruct((rows, dim)...  12 us

profile of v3, /device:TPU:113, one launch (start us, length us, event | category | flops | bytes accessed | tf_op | source)
XLA Modules:
  0.0 136.0 jit_solution(17408797168051293489)
XLA Ops:
  0.6 123.4 %decode_layers.1 = (bf16[32,4096]{1,0:T(8,128)(2,1)}, bf16[4,256,128]{2,1,0:T(8,128)(2,1)}, bf16[4,256,128]{2,1,0:T(8,128)(2,1)}) custom-call(s32[32]{0:T(128)} %lens_ref.3, bf16[32,4096]{1,0:T(8,128)(2,1)} %hid_ref.1, bf16[4,4096,4096]{2,1,0:T(8,128)(2,1)} %wq.1, bf16[4,4096,1024]{2,1,0:T(8,128)(2,1)} %wk.1, bf16[4,4096,1024]{2,1,0:T(8,128)(2,1)} %wv.1, ...), custom_call_target="tpu_custom_call" | custom-call | tf_op jit(solution)/shard_map/decode_layers/pallas_call | solution.py:496
  124.0 12.0 %insert_rows.1 = (bf16[32,4096]{1,0:T(8,128)(2,1)}, bf16[4,32,32,8,128]{4,3,2,1,0:T(8,128)(2,1)}, bf16[4,32,32,8,128]{4,3,2,1,0:T(8,128)(2,1)}) custom-call(s32[32]{0:T(128)} %lens_ref.3, bf16[32,4096]{1,0:T(8,128)(2,1)} %get-tuple-element.6.hid_ref, bf16[4,32,8,128]{3,2,1,0:T(8,128)(2,1)} %bitcast.10, bf16[4,32,8,128]{3,2,1,0:T(8,128)(2,1)} %bitcast.11, ...), custom_call_target="tpu_custom_call" | custom-call | tf_op jit(solution)/shard_map/insert_rows/pallas_call | solution.py:548

commit v4 on v3

--- a/solution.py
+++ b/solution.py
@@ -129,14 +129,16 @@
         return (pltpu.make_async_copy(ks.at[lyr], sfx.at[0], sfx_sem.at[0]),
                 pltpu.make_async_copy(vs.at[lyr], sfx.at[1], sfx_sem.at[1]))
 
+    own_x = pltpu.make_async_copy(hid_ref, xbuf.at[0, my_rows], x0_sem.at[2])
+    own_x.start()
     for cp in raw_copies(0):
         cp.start()
     issue_weights(jnp.int32(0))
     barrier = pltpu.get_barrier_semaphore()
     for j in range(1, n_ctx):
         pl.semaphore_signal(barrier, inc=1, device_id={'ctx': (me + j) % n_ctx}, device_id_type=MESH)
-    xbuf[0, my_rows, :] = hid_ref[...]
     pl.semaphore_wait(barrier, n_ctx - 1)
+    own_x.wait()
     x0 = pltpu.make_async_remote_copy(xbuf.at[0, my_rows], xbuf.at[0, my_rows], x0_sem.at[0], x0_sem.at[1],
                                       device_id={'ctx': mate}, device_id_type=MESH)
     x0.start()
@@ -305,6 +307,8 @@
             cp.wait()
         nh = kvh * grp
         cols = slots * kvh
+        l3[...] = jnp.zeros_like(l3)
+        lane = lax.broadcasted_iota(jnp.int32, (nh, hd), 1)
         slot_id = lax.broadcasted_iota(jnp.int32, (slots, kvh, hd), 0)
         col_id = lax.broadcasted_iota(jnp.int32, (nh, cols), 1)
         row_id = lax.broadcasted_iota(jnp.int32, (nh, cols), 0)
@@ -334,7 +338,10 @@
             os = [jnp.dot(e.astype(BF16), kv[2 * u + 1], preferred_element_type=F32) for u, e in enumerate(es)]
             for at, m, mass, o in zip(ats, ms, sums, os):
                 o3[at, :] = o / mass
-                l3[at, :] = jnp.broadcast_to(m + jnp.log(mass), (nh, hd))
+            part = l3[...]
+            for b, m, mass in zip(bs, ms, sums):
+                part = jnp.where(lane == b, m + jnp.log(mass), part)
+            l3[...] = part
             return 0
 
         lax.fori_loop(0, early, suffix, 0)
@@ -359,33 +366,30 @@
             for cp in sfx_copies(lyr + 1):
                 cp.start()
 
-        def arrived(kind, h):
-            @pl.when((my_head, far_head)[kind] != h)
-            def _():
-                pltpu.make_async_remote_copy(osend.at[0, 0, 0], orecv.at[kind, h], o_ssem.at[0, 0, 0], o_rsem.at[kind, h],
-                                             device_id={'ctx': mate}, device_id_type=MESH).wait_recv()
-                pltpu.make_async_remote_copy(lsend.at[0, 0, 0], lrecv.at[kind, h], l_ssem.at[0, 0, 0], l_rsem.at[kind, h],
-                                             device_id={'ctx': mate}, device_id_type=MESH).wait_recv()
-            return jnp.transpose(jnp.concatenate([lrecv[kind, h]] * (hd // 8), axis=0))
-
         for kind in (1, 0):
             for h in range(kvh):
-                lp = arrived(kind, h)
-                for g in range(grp):
-                    hx = h * grp + g
-                    at = pl.ds(hx, rows, stride=kvh * grp)
-                    la = lp[g * rows:(g + 1) * rows]
-                    ls = l3[at, :]
-                    top = jnp.maximum(la, ls)
-                    wa = jnp.exp(la - top)
-                    ws = jnp.exp(ls - top)
-                    both_mass = wa + ws
-                    mix = (wa * orecv[kind, h, :, g * hd:(g + 1) * hd].astype(F32) + ws * o3[at, :]) / both_mass
-                    if kind:
-                        o3[at, :] = mix
-                        l3[at, :] = top + jnp.log(both_mass)
-                    else:
-                        obuf[my_rows, hx * hd:(hx + 1) * hd] = mix.astype(BF16)
+                @pl.when((my_head, far_head)[kind] != h)
+                def _():
+                    pltpu.make_async_remote_copy(osend.at[0, 0, 0], orecv.at[kind, h], o_ssem.at[0, 0, 0], o_rsem.at[kind, h],
+                                                 device_id={'ctx': mate}, device_id_type=MESH).wait_recv()
+                    pltpu.make_async_remote_copy(lsend.at[0, 0, 0], lrecv.at[kind, h], l_ssem.at[0, 0, 0], l_rsem.at[kind, h],
+                                                 device_id={'ctx': mate}, device_id_type=MESH).wait_recv()
+        parts = [jnp.concatenate([lrecv[kind, h, 0:1] for h in range(kvh)], axis=0) for kind in range(2)]
+        own = l3[pl.ds(0, kvh, stride=grp), :]
+        for g in range(1, grp):
+            own = own + pltpu.roll(l3[pl.ds(g, kvh, stride=grp), :], g * rows, 1)
+        parts.append(own)
+        top = jnp.maximum(jnp.maximum(parts[0], parts[1]), parts[2])
+        ups = [jnp.exp(x - top) for x in parts]
+        inv = 1.0 / (ups[0] + ups[1] + ups[2])
+        turn = jnp.transpose(jnp.concatenate([u * inv for u in ups] + [jnp.zeros((hd - 3 * kvh, hd), F32)], axis=0))
+        for h in range(kvh):
+            for g in range(grp):
+                hx = h * grp + g
+                wt = [turn[g * rows:(g + 1) * rows, i * kvh + h:i * kvh + h + 1] for i in range(3)]
+                mix = (wt[0] * orecv[0, h, :, g * hd:(g + 1) * hd].astype(F32) + wt[1] * orecv[1, h, :, g * hd:(g + 1) * hd].astype(F32)
+                       + wt[2] * o3[pl.ds(hx, rows, stride=kvh * grp), :])
+                obuf[my_rows, hx * hd:(hx + 1) * hd] = mix.astype(BF16)
         ob = pltpu.make_async_remote_copy(obuf.at[my_rows], obuf.at[my_rows], ob_sem.at[0], ob_sem.at[1],
                                           device_id={'ctx': mate}, device_id_type=MESH)
         ob.start()
@@ -498,7 +502,7 @@
             out_shape=(jax.ShapeDtypeStruct((rows, dim), BF16),
                        jax.ShapeDtypeStruct((layers, rows * kvh, hd), BF16),
                        jax.ShapeDtypeStruct((layers, rows * kvh, hd), BF16)),
-            in_specs=[pl.BlockSpec(memory_space=smem), pl.BlockSpec(memory_space=vmem)] + [pl.BlockSpec(memory_space=anys)] * 8,
+            in_specs=[pl.BlockSpec(memory_space=smem)] + [pl.BlockSpec(memory_space=anys)] * 9,
             out_specs=[pl.BlockSpec(memory_space=vmem)] * 3,
             scratch_shapes=[
                 vmem((nslot, dim, qw), BF16),
@@ -520,12 +524,12 @@
                 vmem((rows * nh, hd), F32),
                 vmem((2, rows * kvh, hd), F32),
                 vmem((rows * nh, hd), F32),
-                vmem((rows * nh, hd), F32),
+                vmem((nh, hd), F32),
                 vmem((2 * rows, nh * hd), BF16),
                 pltpu.SemaphoreType.DMA((nslot,)),
                 pltpu.SemaphoreType.DMA((2,)),
                 pltpu.SemaphoreType.DMA((2,)),
-                pltpu.SemaphoreType.DMA((2,)),
+                pltpu.SemaphoreType.DMA((3,)),
                 pltpu.SemaphoreType.DMA((2, chips)),
                 pltpu.SemaphoreType.DMA((2, chips)),
                 pltpu.SemaphoreType.DMA((2,)),

time: 136 us -> 135 us (level)
  no operation moved by 1% of the time
where the time goes in v4:
time: 135 us
  Pallas kernels  134 us (99%)
    pallas_call x1, Pallas kernels, local_step(): pl.pallas_call(functools.partial(decode_kernel, cfg), out_shape=(jax.Shap...  122 us
    pallas_call x1, Pallas kernels, local_step(): pl.pallas_call(insert_kernel, out_shape=(jax.ShapeDtypeStruct((rows, dim)...  12 us

profile of v4, /device:TPU:113, one launch (start us, length us, event | category | flops | bytes accessed | tf_op | source)
XLA Modules:
  0.0 135.1 jit_solution(9631855761127368659)
XLA Ops:
  0.6 122.4 %decode_layers.1 = (bf16[32,4096]{1,0:T(8,128)(2,1)}, bf16[4,256,128]{2,1,0:T(8,128)(2,1)}, bf16[4,256,128]{2,1,0:T(8,128)(2,1)}) custom-call(s32[32]{0:T(128)} %lens_ref.3, bf16[32,4096]{1,0:T(8,128)(2,1)} %hid_ref.1, bf16[4,4096,4096]{2,1,0:T(8,128)(2,1)} %wq.1, bf16[4,4096,1024]{2,1,0:T(8,128)(2,1)} %wk.1, bf16[4,4096,1024]{2,1,0:T(8,128)(2,1)} %wv.1, ...), custom_call_target="tpu_custom_call" | custom-call | tf_op jit(solution)/shard_map/decode_layers/pallas_call | solution.py:500
  123.0 12.0 %insert_rows.1 = (bf16[32,4096]{1,0:T(8,128)(2,1)}, bf16[4,32,32,8,128]{4,3,2,1,0:T(8,128)(2,1)}, bf16[4,32,32,8,128]{4,3,2,1,0:T(8,128)(2,1)}) custom-call(s32[32]{0:T(128)} %lens_ref.3, bf16[32,4096]{1,0:T(8,128)(2,1)} %get-tuple-element.6.hid_ref, bf16[4,32,8,128]{3,2,1,0:T(8,128)(2,1)} %bitcast.10, bf16[4,32,8,128]{3,2,1,0:T(8,128)(2,1)} %bitcast.11, ...), custom_call_target="tpu_custom_call" | custom-call | tf_op jit(solution)/shard_map/insert_rows/pallas_call | solution.py:552
